TPU v7x, 256 devices: a whole 4x4x8 slice. The times are simulated.
256 devices in a mesh: tm: 16 (over y, x), lat: 16 (over z, core).
Axes of the slice: x: 4, y: 4, z: 8, core: 2. Of those that a mesh axis runs over, the one named last changes fastest.
Arguments:
- states: float32 [32, 69, 64, 256], P('tm', None, 'lat'), may hold values from -6 to 6
- observed: float32 [32, 69, 64, 256], P('tm', None, 'lat'), may hold values from -6 to 6
- conv_in: bfloat16 [3, 3, 256, 345], replicated, may hold values from -0.109375 to 0.109375
- bias_in: float32 [256], replicated, may hold values from -3 to 3
- conv_out: bfloat16 [3, 3, 69, 256], replicated, may hold values from -0.125 to 0.125
- bias_out: float32 [69], replicated, may hold values from -3 to 3
Outputs:
- scores: float32 [32, 69, 64, 256], P('tm', None, 'lat')
- guidance: float32 [32, 69, 64, 256], P('tm', None, 'lat')
All inputs are finite; a program needn't handle non-finite values.
Results may differ from a plain program's by a relative error of at most 0.0045.
Values may be sent and summed in bfloat16 or wider, within the bound.
A program may use at most 64 MiB of HBM per device.

v0:
```python
import jax
import jax.numpy as jnp
from jax import lax
from jax.sharding import PartitionSpec as P

WINDOW = 5


def with_halo(block, sides, width, periodic):
    for axis, dim in sides:
        count = lax.axis_size(axis)
        forward = [(i, i + 1) for i in range(count - 1)]
        if periodic:
            forward.append((count - 1, 0))
        backward = [(target, source) for source, target in forward]
        low = lax.ppermute(
            lax.slice_in_dim(block, block.shape[dim] - width, None, axis=dim), axis, forward
        )
        high = lax.ppermute(lax.slice_in_dim(block, 0, width, axis=dim), axis, backward)
        block = jnp.concatenate([low, block, high], axis=dim)
    return block


def from_behind(value, axis, steps):
    count = lax.axis_size(axis)
    pairs = [(source, (source + steps) % count) for source in range(count)]
    return lax.ppermute(value, axis, pairs)


def convolve(padded, weights):
    rows = padded.shape[2] - 2
    total = None
    for j in range(3):
        moved = jnp.roll(padded, 1 - j, axis=3)
        for i in range(3):
            band = moved[:, :, i : i + rows, :]
            term = jnp.einsum(
                "oc,tcrw->torw", weights[i, j], band, preferred_element_type=jnp.float32
            )
            total = term if total is None else total + term
    return total


def flipped(weights):
    return jnp.transpose(weights[::-1, ::-1], (0, 1, 3, 2))


def silu_slope(value):
    sig = jax.nn.sigmoid(value)
    return sig * (1.0 + value * (1.0 - sig))


def gather_windows(extended, count):
    return jnp.concatenate([extended[k : k + count] for k in range(WINDOW)], axis=1)


def shards(states, observed, conv_in, bias_in, conv_out, bias_out):
    count = states.shape[0]
    chans = states.shape[1]
    rows = states.shape[2]
    width = states.shape[3]
    back_in = flipped(conv_in)
    back_out = flipped(conv_out)
    cast = states.astype(jnp.bfloat16)
    extended = with_halo(cast, (("tm", 0),), 2, True)
    bias_hidden = bias_in[None, :, None, None]
    bias_score = bias_out[None, :, None, None]
    widened = with_halo(extended, (("lat", 2),), 1, False)
    windows = gather_windows(widened, count)
    pre = convolve(windows, conv_in) + bias_hidden
    act = jax.nn.silu(pre).astype(jnp.bfloat16)
    act_wide = with_halo(act, (("lat", 2),), 1, False)
    scores = convolve(act_wide, conv_out) + bias_score
    resid = (scores - observed).astype(jnp.bfloat16)
    resid_wide = with_halo(resid, (("lat", 2),), 1, False)
    grad_act = convolve(resid_wide, back_out)
    grad_pre = (grad_act * silu_slope(pre)).astype(jnp.bfloat16)
    grad_wide = with_halo(grad_pre, (("lat", 2),), 1, False)
    grad_window = convolve(grad_wide, back_in)
    slots = grad_window.reshape(count, WINDOW, chans, rows, width)
    gathered = None
    for k in range(WINDOW):
        placed = jnp.pad(slots[:, k], ((k, WINDOW - 1 - k), (0, 0), (0, 0), (0, 0)))
        gathered = placed if gathered is None else gathered + placed
    owned = gathered[2 : count + 2]
    from_next = from_behind(gathered[:2].astype(jnp.bfloat16), "tm", -1).astype(jnp.float32)
    from_prev = from_behind(gathered[count + 2 :].astype(jnp.bfloat16), "tm", 1).astype(jnp.float32)
    guidance = owned + from_next
    guidance = guidance + from_prev
    return (scores, guidance)


def solution(mesh):
    in_specs = (P("tm", None, "lat", None), P("tm", None, "lat", None), P(), P(), P(), P())
    out_specs = (P("tm", None, "lat", None), P("tm", None, "lat", None))
    return jax.shard_map(shards, mesh=mesh, in_specs=in_specs, out_specs=out_specs, check_vma=False)
```

profile of v0, /device:TPU:97, one launch (start us, length us, event | category | flops | bytes accessed | tf_op | source)
XLA Modules:
  0.0 118.7 jit_solution(5408218284324575588)
XLA Ops:
  1.9 5.0 %collective-permute-start.1 = (bf16[2,69,4,256]{3,1,2,0:T(8,128)(2,1)S(1)}, bf16[2,69,4,256]{3,1,2,0:T(8,128)(2,1)S(1)}, u32[]{:S(2)}, u32[]{:S(2)}) collective-permute-start(bf16[2,69,4,256]{3,1,2,0:T(8,128)(2,1)S(1)} %copy.122), channel_id=1, source_target_pairs={{16,0},{32,16},{48,32},{64,48},{80,64},{96,80},{112,96},{128,112},... | collective-permute-start | bytes 847880 | tf_op jit(solution)/shard_map/ppermute | solution.py:19
  7.0 5.7 %collective-permute-done.1 = bf16[2,69,4,256]{3,1,2,0:T(8,128)(2,1)S(1)} collective-permute-done((bf16[2,69,4,256]{3,1,2,0:T(8,128)(2,1)S(1)}, bf16[2,69,4,256]{3,1,2,0:T(8,128)(2,1)S(1)}, u32[]{:S(2)}, u32[]{:S(2)}) %collective-permute-start.1) | collective-permute-done | bytes 282656 | tf_op jit(solution)/shard_map/ppermute | solution.py:19
  12.6 5.2 %collective-permute-done = bf16[2,69,4,256]{3,1,2,0:T(8,128)(2,1)S(1)} collective-permute-done((bf16[2,69,4,256]{3,1,2,0:T(8,128)(2,1)S(1)}, bf16[2,69,4,256]{3,1,2,0:T(8,128)(2,1)S(1)}, u32[]{:S(2)}, u32[]{:S(2)}) %collective-permute-start) | collective-permute-done | bytes 282656 | tf_op jit(solution)/shard_map/ppermute | solution.py:16
  17.9 6.5 %collective-permute-start.2 = (bf16[6,69,1,256]{3,1,2,0:T(8,128)(2,1)S(1)}, bf16[6,69,1,256]{3,1,2,0:T(8,128)(2,1)S(1)}, u32[]{:S(2)}, u32[]{:S(2)}) collective-permute-start(bf16[6,69,1,256]{3,1,2,0:T(8,128)(2,1)S(1)} %get-tuple-element.32), channel_id=1, source_target_pairs={{0,1},{1,2},{2,3},{3,4},{4,5},{5,6},{6,7},{7,8},{8,9},{9,10},{10,1... | collective-permute-start | bytes 635912 | tf_op jit(solution)/shard_map/ppermute | solution.py:16
  24.4 1.9 %collective-permute-start.3 = (bf16[6,69,1,256]{3,1,2,0:T(8,128)(2,1)S(1)}, bf16[6,69,1,256]{3,1,2,0:T(8,128)(2,1)S(1)}, u32[]{:S(2)}, u32[]{:S(2)}) collective-permute-start(bf16[6,69,1,256]{3,1,2,0:T(8,128)(2,1)S(1)} %get-tuple-element.33), channel_id=1, source_target_pairs={{1,0},{2,1},{3,2},{4,3},{5,4},{6,5},{7,6},{8,7},{9,8},{10,9},{11,1... | collective-permute-start | bytes 635912 | tf_op jit(solution)/shard_map/ppermute | solution.py:19
  28.4 4.5 %collective-permute-done.3 = bf16[6,69,1,256]{3,1,2,0:T(8,128)(2,1)S(1)} collective-permute-done((bf16[6,69,1,256]{3,1,2,0:T(8,128)(2,1)S(1)}, bf16[6,69,1,256]{3,1,2,0:T(8,128)(2,1)S(1)}, u32[]{:S(2)}, u32[]{:S(2)}) %collective-permute-start.3) | collective-permute-done | bytes 212000 | tf_op jit(solution)/shard_map/ppermute | solution.py:19
  34.1 6.8 %concatenate.68 = bf16[2,345,6,256]{3,1,2,0:T(8,128)(2,1)S(1)} concatenate(bf16[2,69,6,256]{3,1,2,0:T(8,128)(2,1)} %get-tuple-element.27, bf16[2,69,6,256]{3,1,2,0:T(8,128)(2,1)} %get-tuple-element.26, bf16[2,69,6,256]{3,1,2,0:T(8,128)(2,1)S(1)} %get-tuple-element.25, bf16[2,69,6,256]{3,1,2,0:T(8,128)(2,1)S(1)} %get-tuple-element.24, bf16[2,69,6,256]{3,1,2,0:T(8,128)(2,1)S(1)} %get-tuple-element.23), dimensions={1} | concatenate | bytes 4239360 | tf_op jit(solution)/shard_map/concatenate | solution.py:54
  41.0 1.8 %fusion.59 = f32[2,4,256,256]{3,2,1,0:T(8,128)S(1)} fusion(bf16[2,345,6,256]{3,1,2,0:T(8,128)(2,1)S(1)} %concatenate.68, bf16[3,3,256,345]{2,3,1,0:T(8,128)(2,1)} %param.8), kind=kOutput, calls=%fused_computation.105 | convolution fusion | flops 361758720 | bytes 4397056 | tf_op jit(solution)/shard_map/oc,tcrw->torw/dot_general | solution.py:37
  52.4 1.7 %fusion.4 = (bf16[2,256,4,256]{1,3,2,0:T(8,128)(2,1)S(1)}, f32[2,4,256,256]{3,2,1,0:T(8,128)S(1)}) fusion(f32[256]{0:T(256)S(1)} %copy-done.7, f32[2,4,256,256]{3,2,1,0:T(8,128)S(1)} %fusion.52, f32[2,4,256,256]{3,2,1,0:T(8,128)S(1)} %fusion.54, f32[2,4,256,256]{3,2,1,0:T(8,128)S(1)} %fusion.56, bf16[2,345,6,256]{3,1,2,0:T(8,128)(2,1)S(1)} %concatenate.68, ...), kind=kOutput, calls=%fused_computation.11 | convolution fusion | flops 369098752 | bytes 22266880 | tf_op jit(solution)/shard_map/oc,tcrw->torw/dot_general | solution.py:37
  54.1 1.9 %collective-permute-start.4 = (bf16[2,256,1,256]{1,3,2,0:T(8,128)(2,1)S(1)}, bf16[2,256,1,256]{1,3,2,0:T(8,128)(2,1)S(1)}, u32[]{:S(2)}, u32[]{:S(2)}) collective-permute-start(bf16[2,256,1,256]{1,3,2,0:T(8,128)(2,1)S(1)} %get-tuple-element.30), channel_id=1, source_target_pairs={{0,1},{1,2},{2,3},{3,4},{4,5},{5,6},{6,7},{7,8},{8,9},{9,10},{10,1... | collective-permute-start | bytes 786440 | tf_op jit(solution)/shard_map/ppermute | solution.py:16
  56.0 2.6 %collective-permute-start.5 = (bf16[2,256,1,256]{1,3,2,0:T(8,128)(2,1)S(1)}, bf16[2,256,1,256]{1,3,2,0:T(8,128)(2,1)S(1)}, u32[]{:S(2)}, u32[]{:S(2)}) collective-permute-start(bf16[2,256,1,256]{1,3,2,0:T(8,128)(2,1)S(1)} %get-tuple-element.31), channel_id=1, source_target_pairs={{1,0},{2,1},{3,2},{4,3},{5,4},{6,5},{7,6},{8,7},{9,8},{10,9},{11,1... | collective-permute-start | bytes 786440 | tf_op jit(solution)/shard_map/ppermute | solution.py:19
  59.3 5.6 %collective-permute-done.5 = bf16[2,256,1,256]{1,3,2,0:T(8,128)(2,1)S(1)} collective-permute-done((bf16[2,256,1,256]{1,3,2,0:T(8,128)(2,1)S(1)}, bf16[2,256,1,256]{1,3,2,0:T(8,128)(2,1)S(1)}, u32[]{:S(2)}, u32[]{:S(2)}) %collective-permute-start.5) | collective-permute-done | bytes 262176 | tf_op jit(solution)/shard_map/ppermute | solution.py:19
  70.4 1.9 %collective-permute-start.6 = (bf16[2,69,1,256]{3,1,2,0:T(8,128)(2,1)S(1)}, bf16[2,69,1,256]{3,1,2,0:T(8,128)(2,1)S(1)}, u32[]{:S(2)}, u32[]{:S(2)}) collective-permute-start(bf16[2,69,1,256]{3,1,2,0:T(8,128)(2,1)S(1)} %get-tuple-element.40), channel_id=1, source_target_pairs={{0,1},{1,2},{2,3},{3,4},{4,5},{5,6},{6,7},{7,8},{8,9},{9,10},{10,1... | collective-permute-start | bytes 211976 | tf_op jit(solution)/shard_map/ppermute | solution.py:16
  72.4 2.4 %collective-permute-start.7 = (bf16[2,69,1,256]{3,1,2,0:T(8,128)(2,1)S(1)}, bf16[2,69,1,256]{3,1,2,0:T(8,128)(2,1)S(1)}, u32[]{:S(2)}, u32[]{:S(2)}) collective-permute-start(bf16[2,69,1,256]{3,1,2,0:T(8,128)(2,1)S(1)} %get-tuple-element.41), channel_id=1, source_target_pairs={{1,0},{2,1},{3,2},{4,3},{5,4},{6,5},{7,6},{8,7},{9,8},{10,9},{11,1... | collective-permute-start | bytes 211976 | tf_op jit(solution)/shard_map/ppermute | solution.py:19
  75.3 4.0 %collective-permute-done.7 = bf16[2,69,1,256]{3,1,2,0:T(8,128)(2,1)S(1)} collective-permute-done((bf16[2,69,1,256]{3,1,2,0:T(8,128)(2,1)S(1)}, bf16[2,69,1,256]{3,1,2,0:T(8,128)(2,1)S(1)}, u32[]{:S(2)}, u32[]{:S(2)}) %collective-permute-start.7) | collective-permute-done | bytes 70688 | tf_op jit(solution)/shard_map/ppermute | solution.py:19
  84.5 1.5 %fusion = bf16[2,256,4,256]{1,3,2,0:T(8,128)(2,1)S(1)} fusion(f32[2,4,256,256]{3,2,1,0:T(8,128)S(1)} %get-tuple-element.43, f32[2,4,256,256]{3,2,1,0:T(8,128)S(1)} %fusion.78, f32[2,4,256,256]{3,2,1,0:T(8,128)S(1)} %fusion.79, f32[2,4,256,256]{3,2,1,0:T(8,128)S(1)} %fusion.80, f32[2,4,256,256]{3,2,1,0:T(8,128)S(1)} %fusion.81, ...), kind=kOutput, calls=%fused_computation.4 | convolution fusion | flops 81971200 | bytes 20328448 | tf_op jit(solution)/shard_map/oc,tcrw->torw/dot_general | solution.py:37
  86.1 1.9 %collective-permute-start.8 = (bf16[2,256,1,256]{1,3,2,0:T(8,128)(2,1)S(1)}, bf16[2,256,1,256]{1,3,2,0:T(8,128)(2,1)S(1)}, u32[]{:S(2)}, u32[]{:S(2)}) collective-permute-start(bf16[2,256,1,256]{1,3,2,0:T(8,128)(2,1)S(1)} %get-tuple-element.28), channel_id=1, source_target_pairs={{0,1},{1,2},{2,3},{3,4},{4,5},{5,6},{6,7},{7,8},{8,9},{9,10},{10,1... | collective-permute-start | bytes 786440 | tf_op jit(solution)/shard_map/ppermute | solution.py:16
  88.1 2.6 %collective-permute-start.9 = (bf16[2,256,1,256]{1,3,2,0:T(8,128)(2,1)S(1)}, bf16[2,256,1,256]{1,3,2,0:T(8,128)(2,1)S(1)}, u32[]{:S(2)}, u32[]{:S(2)}) collective-permute-start(bf16[2,256,1,256]{1,3,2,0:T(8,128)(2,1)S(1)} %get-tuple-element.29), channel_id=1, source_target_pairs={{1,0},{2,1},{3,2},{4,3},{5,4},{6,5},{7,6},{8,7},{9,8},{10,9},{11,1... | collective-permute-start | bytes 786440 | tf_op jit(solution)/shard_map/ppermute | solution.py:19
  90.7 2.1 %fusion.48 = f32[2,4,256,345]{2,3,1,0:T(8,128)} fusion(bf16[2,256,4,256]{1,3,2,0:T(8,128)(2,1)S(1)} %fusion, bf16[3,3,345,256]{3,2,1,0:T(8,128)(2,1)S(1)} %copy-done.2), kind=kOutput, calls=%fused_computation.90 | convolution fusion | flops 361758720 | bytes 4055040 | tf_op jit(solution)/shard_map/oc,tcrw->torw/dot_general | solution.py:37
  92.9 4.1 %collective-permute-done.9 = bf16[2,256,1,256]{1,3,2,0:T(8,128)(2,1)S(1)} collective-permute-done((bf16[2,256,1,256]{1,3,2,0:T(8,128)(2,1)S(1)}, bf16[2,256,1,256]{1,3,2,0:T(8,128)(2,1)S(1)}, u32[]{:S(2)}, u32[]{:S(2)}) %collective-permute-start.9) | collective-permute-done | bytes 262176 | tf_op jit(solution)/shard_map/ppermute | solution.py:19
  101.8 2.8 %add_bitcast_fusion = f32[2,345,4,256]{3,1,2,0:T(8,128)S(1)} fusion(f32[2,4,256,345]{2,3,1,0:T(8,128)S(1)} %fusion.46, f32[2,4,256,345]{2,3,1,0:T(8,128)S(1)} %fusion.47, f32[2,4,256,345]{2,3,1,0:T(8,128)S(1)} %fusion.23, f32[2,4,256,345]{2,3,1,0:T(8,128)} %fusion.48, f32[2,4,256,345]{2,3,1,0:T(8,128)S(1)} %fusion.19, f32[2,4,256,345]{2,3,1,0:T(8,128)S(1)} %fusion.49, ...), kind=kOutput, calls=%fused_computation | convolution fusion | flops 373702656 | bytes 28813312 | tf_op jit(solution)/shard_map/oc,tcrw->torw/dot_general | solution.py:37
  104.6 1.8 %copy.54 = f32[2,345,4,256]{3,2,1,0:T(4,128)S(1)} copy(f32[2,345,4,256]{3,1,2,0:T(8,128)S(1)} %add_bitcast_fusion) | data formatting | bytes 5652480 | tf_op jit(solution)/shard_map/add | solution.py:40
  110.2 4.1 %collective-permute-done.10 = bf16[2,69,4,256]{3,2,1,0:T(4,128)(2,1)S(1)} collective-permute-done((bf16[2,69,4,256]{3,2,1,0:T(4,128)(2,1)S(1)}, bf16[2,69,4,256]{3,2,1,0:T(4,128)(2,1)S(1)}, u32[]{:S(2)}, u32[]{:S(2)}) %collective-permute-start.10) | collective-permute-done | bytes 282656 | tf_op jit(solution)/shard_map/ppermute | solution.py:27
  114.3 3.3 %collective-permute-done.11 = bf16[2,69,4,256]{3,2,1,0:T(4,128)(2,1)S(1)} collective-permute-done((bf16[2,69,4,256]{3,2,1,0:T(4,128)(2,1)S(1)}, bf16[2,69,4,256]{3,2,1,0:T(4,128)(2,1)S(1)}, u32[]{:S(2)}, u32[]{:S(2)}) %collective-permute-start.11) | collective-permute-done | bytes 282656 | tf_op jit(solution)/shard_map/ppermute | solution.py:27
  (80 shorter events, 35.7 us)
Async XLA Ops:
  0.6 25.7 %copy-start.4 = (bf16[3,3,69,256]{3,2,1,0:T(8,128)(2,1)S(1)}, bf16[3,3,69,256]{3,2,1,0:T(8,128)(2,1)}, u32[]{:S(2)}) copy-start(bf16[3,3,69,256]{3,2,1,0:T(8,128)(2,1)} %param.10) | copy-start | bytes 953860
  0.6 26.4 %copy-start = (bf16[3,3,256,345]{2,3,1,0:T(8,128)(2,1)S(1)}, bf16[3,3,256,345]{2,3,1,0:T(8,128)(2,1)}, u32[]{:S(2)}) copy-start(bf16[3,3,256,345]{2,3,1,0:T(8,128)(2,1)} %param.8) | copy-start | bytes 4769284
  1.9 10.7 %collective-permute-start.1 = (bf16[2,69,4,256]{3,1,2,0:T(8,128)(2,1)S(1)}, bf16[2,69,4,256]{3,1,2,0:T(8,128)(2,1)S(1)}, u32[]{:S(2)}, u32[]{:S(2)}) collective-permute-start(bf16[2,69,4,256]{3,1,2,0:T(8,128)(2,1)S(1)} %copy.122), channel_id=1, source_target_pairs={{16,0},{32,16},{48,32},{64,48},{80,64},{96,80},{112,96},{128,112},... | collective-permute-start | bytes 847880 | tf_op jit(solution)/shard_map/ppermute | solution.py:19
  6.9 10.9 %collective-permute-start = (bf16[2,69,4,256]{3,1,2,0:T(8,128)(2,1)S(1)}, bf16[2,69,4,256]{3,1,2,0:T(8,128)(2,1)S(1)}, u32[]{:S(2)}, u32[]{:S(2)}) collective-permute-start(bf16[2,69,4,256]{3,1,2,0:T(8,128)(2,1)S(1)} %copy.122), channel_id=1, source_target_pairs={{0,16},{16,32},{32,48},{48,64},{64,80},{80,96},{96,112},{112,128},... | collective-permute-start | bytes 847880 | tf_op jit(solution)/shard_map/ppermute | solution.py:16
  17.9 10.4 %collective-permute-start.2 = (bf16[6,69,1,256]{3,1,2,0:T(8,128)(2,1)S(1)}, bf16[6,69,1,256]{3,1,2,0:T(8,128)(2,1)S(1)}, u32[]{:S(2)}, u32[]{:S(2)}) collective-permute-start(bf16[6,69,1,256]{3,1,2,0:T(8,128)(2,1)S(1)} %get-tuple-element.32), channel_id=1, source_target_pairs={{0,1},{1,2},{2,3},{3,4},{4,5},{5,6},{6,7},{7,8},{8,9},{9,10},{10,1... | collective-permute-start | bytes 635912 | tf_op jit(solution)/shard_map/ppermute | solution.py:16
  24.4 8.5 %collective-permute-start.3 = (bf16[6,69,1,256]{3,1,2,0:T(8,128)(2,1)S(1)}, bf16[6,69,1,256]{3,1,2,0:T(8,128)(2,1)S(1)}, u32[]{:S(2)}, u32[]{:S(2)}) collective-permute-start(bf16[6,69,1,256]{3,1,2,0:T(8,128)(2,1)S(1)} %get-tuple-element.33), channel_id=1, source_target_pairs={{1,0},{2,1},{3,2},{4,3},{5,4},{6,5},{7,6},{8,7},{9,8},{10,9},{11,1... | collective-permute-start | bytes 635912 | tf_op jit(solution)/shard_map/ppermute | solution.py:19
  41.0 1.8 %copy-start.1 = (bf16[3,3,256,345]{2,3,1,0:T(8,128)(2,1)S(1)}, bf16[3,3,256,345]{2,3,1,0:T(8,128)(2,1)}, u32[]{:S(2)}) copy-start(bf16[3,3,256,345]{2,3,1,0:T(8,128)(2,1)} %param.8) | copy-start | bytes 4769284
  51.3 1.0 copy-start.7
  52.3 6.3 %copy-start.5 = (bf16[3,3,69,256]{3,2,1,0:T(8,128)(2,1)S(1)}, bf16[3,3,69,256]{3,2,1,0:T(8,128)(2,1)}, u32[]{:S(2)}) copy-start(bf16[3,3,69,256]{3,2,1,0:T(8,128)(2,1)} %param.10) | copy-start | bytes 953860
  54.1 5.2 %collective-permute-start.4 = (bf16[2,256,1,256]{1,3,2,0:T(8,128)(2,1)S(1)}, bf16[2,256,1,256]{1,3,2,0:T(8,128)(2,1)S(1)}, u32[]{:S(2)}, u32[]{:S(2)}) collective-permute-start(bf16[2,256,1,256]{1,3,2,0:T(8,128)(2,1)S(1)} %get-tuple-element.30), channel_id=1, source_target_pairs={{0,1},{1,2},{2,3},{3,4},{4,5},{5,6},{6,7},{7,8},{8,9},{9,10},{10,1... | collective-permute-start | bytes 786440 | tf_op jit(solution)/shard_map/ppermute | solution.py:16
  56.0 8.9 %collective-permute-start.5 = (bf16[2,256,1,256]{1,3,2,0:T(8,128)(2,1)S(1)}, bf16[2,256,1,256]{1,3,2,0:T(8,128)(2,1)S(1)}, u32[]{:S(2)}, u32[]{:S(2)}) collective-permute-start(bf16[2,256,1,256]{1,3,2,0:T(8,128)(2,1)S(1)} %get-tuple-element.31), channel_id=1, source_target_pairs={{1,0},{2,1},{3,2},{4,3},{5,4},{6,5},{7,6},{8,7},{9,8},{10,9},{11,1... | collective-permute-start | bytes 786440 | tf_op jit(solution)/shard_map/ppermute | solution.py:19
  68.7 1.1 copy-start.6
  68.7 1.1 copy-start.8
  69.8 5.0 %copy-start.3 = (bf16[3,3,256,69]{2,3,1,0:T(8,128)(2,1)S(1)}, bf16[3,3,256,69]{2,3,1,0:T(8,128)(2,1)}, u32[]{:S(2)}) copy-start(bf16[3,3,256,69]{2,3,1,0:T(8,128)(2,1)} %reverse_bitcast_fusion.1) | copy-start | bytes 953860
  70.4 4.8 %collective-permute-start.6 = (bf16[2,69,1,256]{3,1,2,0:T(8,128)(2,1)S(1)}, bf16[2,69,1,256]{3,1,2,0:T(8,128)(2,1)S(1)}, u32[]{:S(2)}, u32[]{:S(2)}) collective-permute-start(bf16[2,69,1,256]{3,1,2,0:T(8,128)(2,1)S(1)} %get-tuple-element.40), channel_id=1, source_target_pairs={{0,1},{1,2},{2,3},{3,4},{4,5},{5,6},{6,7},{7,8},{8,9},{9,10},{10,1... | collective-permute-start | bytes 211976 | tf_op jit(solution)/shard_map/ppermute | solution.py:16
  72.4 6.9 %collective-permute-start.7 = (bf16[2,69,1,256]{3,1,2,0:T(8,128)(2,1)S(1)}, bf16[2,69,1,256]{3,1,2,0:T(8,128)(2,1)S(1)}, u32[]{:S(2)}, u32[]{:S(2)}) collective-permute-start(bf16[2,69,1,256]{3,1,2,0:T(8,128)(2,1)S(1)} %get-tuple-element.41), channel_id=1, source_target_pairs={{1,0},{2,1},{3,2},{4,3},{5,4},{6,5},{7,6},{8,7},{9,8},{10,9},{11,1... | collective-permute-start | bytes 211976 | tf_op jit(solution)/shard_map/ppermute | solution.py:19
  84.5 6.2 %copy-start.2 = (bf16[3,3,345,256]{3,2,1,0:T(8,128)(2,1)S(1)}, bf16[3,3,345,256]{3,2,1,0:T(8,128)(2,1)}, u32[]{:S(2)}) copy-start(bf16[3,3,345,256]{3,2,1,0:T(8,128)(2,1)} %reverse_bitcast_fusion) | copy-start | bytes 4769284
  86.1 6.7 %collective-permute-start.8 = (bf16[2,256,1,256]{1,3,2,0:T(8,128)(2,1)S(1)}, bf16[2,256,1,256]{1,3,2,0:T(8,128)(2,1)S(1)}, u32[]{:S(2)}, u32[]{:S(2)}) collective-permute-start(bf16[2,256,1,256]{1,3,2,0:T(8,128)(2,1)S(1)} %get-tuple-element.28), channel_id=1, source_target_pairs={{0,1},{1,2},{2,3},{3,4},{4,5},{5,6},{6,7},{7,8},{8,9},{9,10},{10,1... | collective-permute-start | bytes 786440 | tf_op jit(solution)/shard_map/ppermute | solution.py:16
  88.1 8.9 %collective-permute-start.9 = (bf16[2,256,1,256]{1,3,2,0:T(8,128)(2,1)S(1)}, bf16[2,256,1,256]{1,3,2,0:T(8,128)(2,1)S(1)}, u32[]{:S(2)}, u32[]{:S(2)}) collective-permute-start(bf16[2,256,1,256]{1,3,2,0:T(8,128)(2,1)S(1)} %get-tuple-element.29), channel_id=1, source_target_pairs={{1,0},{2,1},{3,2},{4,3},{5,4},{6,5},{7,6},{8,7},{9,8},{10,9},{11,1... | collective-permute-start | bytes 786440 | tf_op jit(solution)/shard_map/ppermute | solution.py:19
  107.6 6.7 %collective-permute-start.10 = (bf16[2,69,4,256]{3,2,1,0:T(4,128)(2,1)S(1)}, bf16[2,69,4,256]{3,2,1,0:T(4,128)(2,1)S(1)}, u32[]{:S(2)}, u32[]{:S(2)}) collective-permute-start(bf16[2,69,4,256]{3,2,1,0:T(4,128)(2,1)S(1)} %get-tuple-element.34), channel_id=1, source_target_pairs={{0,240},{16,0},{32,16},{48,32},{64,48},{80,64},{96,80},{112,96},{1... | collective-permute-start | bytes 847880 | tf_op jit(solution)/shard_map/ppermute | solution.py:27
  107.7 9.9 %collective-permute-start.11 = (bf16[2,69,4,256]{3,2,1,0:T(4,128)(2,1)S(1)}, bf16[2,69,4,256]{3,2,1,0:T(4,128)(2,1)S(1)}, u32[]{:S(2)}, u32[]{:S(2)}) collective-permute-start(bf16[2,69,4,256]{3,2,1,0:T(4,128)(2,1)S(1)} %get-tuple-element.35), channel_id=1, source_target_pairs={{0,16},{16,32},{32,48},{48,64},{64,80},{80,96},{96,112},{112,128},... | collective-permute-start | bytes 847880 | tf_op jit(solution)/shard_map/ppermute | solution.py:27
where the time goes:
time: 119 us
  waiting for transfers between devices  36.8 us (31%)
  matrix products  31.2 us (26%)
  starting transfers between devices  28.3 us (24%)
  local copies, waits for them, and re-layouts  18.2 us (15%)
  other arithmetic  3.02 us (3%)
    dot_general x36, matrix products, convolve(): jnp.einsum('oc,tcrw->torw', weights[i, j], band, preferred_element_type=j...  31.2 us
    ppermute x5, waiting for transfers between devices, with_halo(): lax.ppermute(lax.slice_in_dim(block, 0, width, axis=dim), axis, backward)  23.9 us
    ppermute x5, starting transfers between devices, with_halo(): lax.ppermute(lax.slice_in_dim(block, 0, width, axis=dim), axis, backward)  14.5 us
    ppermute x5, starting transfers between devices, with_halo(): lax.ppermute(lax.slice_in_dim(block, block.shape[dim] - width, None, axis...  12.2 us
    ppermute x2, waiting for transfers between devices, from_behind(): return lax.ppermute(value, axis, pairs)  7.42 us
    concatenate x1, local copies, waits for them, and re-layouts, gather_windows(): jnp.concatenate([extended[k:k + count] for k in range(WINDOW)], axis=1)  6.83 us
    ppermute x5, waiting for transfers between devices, with_halo(): lax.ppermute(lax.slice_in_dim(block, block.shape[dim] - width, None, axis...  5.5 us
    slice x6, local copies, waits for them, and re-layouts, convolve(): moved = jnp.roll(padded, 1 - j, axis=3)  3.21 us
  transfers between devices with their start and end apart: 12, of which 9 were waited for; matrix products, arithmetic and copies ran while one was open for 5% of the time, Pallas kernels for 0%

commit v1 on v0

v1 whole, which is shorter than its diff:
```python
import jax
import jax.numpy as jnp
from jax import lax
from jax.experimental import pallas as pl
from jax.experimental.pallas import tpu as pltpu
from jax.sharding import PartitionSpec as P

MESH = pl.DeviceIdType.MESH
F32 = jnp.float32
BF16 = jnp.bfloat16
C = 69
HID = 256
WINDOW = 5
LON = 256
ROWS = 4
OWN = 2
SPAN = OWN + WINDOW - 1
MAIN = 64
TAIL = 8
STACK = 3 * (MAIN + TAIL)
ZROWS = 224
CHUNK = 2 * MAIN + 2 * TAIL
EDGE = MAIN + 2 * TAIL


def dot(a, b):
    return jnp.dot(a, b, preferred_element_type=F32)


def parts(x):
    tail = jnp.concatenate([x[MAIN:], jnp.zeros((MAIN + TAIL - C, x.shape[1]), F32)], axis=0)
    return x[:MAIN], tail


def left(x):
    return pltpu.roll(x, LON - 1, axis=1)


def right(x):
    return pltpu.roll(x, 1, axis=1)


def stack_into(ref, main, tail, first, last):
    ref[0:64, :] = first(main)
    ref[64:128, :] = main
    ref[128:192, :] = last(main)
    tails = jnp.concatenate([first(tail), tail, last(tail), jnp.zeros((TAIL, LON), F32)], axis=0)
    ref[192:224, :] = tails.astype(BF16)


def combine(z, first, last):
    main = first(z[0:64]) + z[64:128] + last(z[128:192])
    tail = first(z[192:200]) + z[200:208] + last(z[208:216])
    return main, tail


def kernel(
    states, observed, conv_in, bias_in, conv_out, bias_out, scores_out, guidance_out,
    st, ob, wi, wo, w4, w1, w2, w2t, bi, bo, sbuf, rbuf, hb, xs, pre, slope, act, sp, rp, kc, sc,
    rs, gp, sg, rg, own, so, go,
    local, tm_send, tm_recv, lat_send, lat_recv, x2_send, x2_recv, x3_send, x3_recv, g_send, g_recv,
):
    m = lax.axis_index("tm")
    l = lax.axis_index("lat")
    count_m = lax.axis_size("tm")
    count_l = lax.axis_size("lat")
    nxt = lax.rem(m + 1, count_m)
    prv = lax.rem(m + count_m - 1, count_m)
    has_up = l > 0
    has_down = l < count_l - 1

    load_st = pltpu.make_async_copy(states, st, local.at[0])
    load_wi = pltpu.make_async_copy(conv_in, wi, local.at[1])
    load_wo = pltpu.make_async_copy(conv_out, wo, local.at[2])
    load_ob = pltpu.make_async_copy(observed, ob, local.at[3])
    load_st.start()
    load_wi.start()
    load_wo.start()
    load_ob.start()

    barrier = pltpu.get_barrier_semaphore()
    pl.semaphore_signal(barrier, inc=1, device_id=(nxt, l), device_id_type=MESH)
    pl.semaphore_signal(barrier, inc=1, device_id=(prv, l), device_id_type=MESH)

    @pl.when(has_up)
    def _():
        pl.semaphore_signal(barrier, inc=1, device_id=(m, l - 1), device_id_type=MESH)

    @pl.when(has_down)
    def _():
        pl.semaphore_signal(barrier, inc=1, device_id=(m, l + 1), device_id_type=MESH)

    def remote(src, dst, send, recv, where):
        return pltpu.make_async_remote_copy(
            src_ref=src, dst_ref=dst, send_sem=send, recv_sem=recv, device_id=where, device_id_type=MESH
        )

    def tm_copy(d, s, g):
        where = (nxt, l) if d == 0 else (prv, l)
        return remote(sbuf.at[s, g], rbuf.at[d, s, g], tm_send.at[d, s, g], tm_recv.at[d, s, g], where)

    def lat_copy(d, e, chunk):
        if d == 0:
            return remote(chunk.at[pl.ds(MAIN, EDGE)], hb.at[0, e], lat_send.at[0, e], lat_recv.at[0, e], (m, l + 1))
        return remote(chunk.at[pl.ds(0, EDGE)], hb.at[1, e], lat_send.at[1, e], lat_recv.at[1, e], (m, l - 1))

    def chunk_of(e, g):
        if e < OWN:
            return rbuf.at[0, e, g]
        if e < 2 * OWN:
            return sbuf.at[e - OWN, g]
        return rbuf.at[1, e - 2 * OWN, g]

    def lat_start(e):
        @pl.when(has_down)
        def _():
            lat_copy(0, e, chunk_of(e, 0)).start()

        @pl.when(has_up)
        def _():
            lat_copy(1, e, chunk_of(e, 0)).start()

    def x2_copy(d):
        where = (m, l + 1) if d == 0 else (m, l - 1)
        return remote(sp.at[d], rp.at[d], x2_send.at[d], x2_recv.at[d], where)

    def x3_copy(d):
        if d == 0:
            return remote(gp.at[4], gp.at[0], x3_send.at[0], x3_recv.at[0], (m, l + 1))
        return remote(gp.at[1], gp.at[5], x3_send.at[1], x3_recv.at[1], (m, l - 1))

    def g_copy(d, r):
        where = (nxt, l) if d == 0 else (prv, l)
        return remote(sg.at[d, r], rg.at[d, r], g_send.at[d, r], g_recv.at[d, r], where)

    load_st.wait()
    for g, (a, b) in enumerate(((0, 3), (1, 2))):
        for s in range(OWN):
            main_a, tail_a = parts(st[s, :, a, :])
            main_b, tail_b = parts(st[s, :, b, :])
            sbuf[s, g, 0:64, :] = main_a.astype(BF16)
            sbuf[s, g, 64:80, :] = jnp.concatenate([tail_a, tail_b], axis=0).astype(BF16)
            sbuf[s, g, 80:144, :] = main_b.astype(BF16)
        if g == 0:
            pl.semaphore_wait(barrier, 2 + has_up.astype(jnp.int32) + has_down.astype(jnp.int32))

        tm_copy(0, 1, g).start()
        tm_copy(1, 0, g).start()
        tm_copy(0, 0, g).start()
        tm_copy(1, 1, g).start()
        if g == 0:
            for s in range(OWN):
                lat_start(OWN + s)

    def zero_pads(n, carry):
        xs[n // SPAN, lax.rem(n, SPAN), ZROWS:256, :] = jnp.zeros((256 - ZROWS, LON), BF16)
        return carry

    lax.fori_loop(0, (ROWS + 2) * SPAN, zero_pads, 0)
    for rho in range(ROWS + 2):
        for t in range(OWN):
            rs[rho, t, ZROWS:256, :] = jnp.zeros((256 - ZROWS, LON), BF16)

    def zero_halo(rho):
        def one(e, carry):
            xs[rho, e, 0:ZROWS, :] = jnp.zeros((ZROWS, LON), BF16)
            return carry

        lax.fori_loop(0, SPAN, one, 0)
        for t in range(OWN):
            rs[rho, t, 0:ZROWS, :] = jnp.zeros((ZROWS, LON), BF16)
            gp[rho, t] = jnp.zeros((HID, LON), BF16)

    @pl.when(jnp.logical_not(has_up))
    def _():
        zero_halo(0)

    @pl.when(jnp.logical_not(has_down))
    def _():
        zero_halo(ROWS + 1)

    bi[...] = jnp.broadcast_to(bias_in[...][None, :], (HID, HID)).T
    row = jnp.concatenate([bias_out[...][None, :], jnp.zeros((1, 128 - C), F32)], axis=1)
    column = jnp.broadcast_to(row, (128, 128)).T
    bo[...] = jnp.concatenate([column[: MAIN + TAIL], column[: MAIN + TAIL]], axis=1)

    load_wi.wait()

    def weights(i, carry):
        for k in range(WINDOW):
            tails = []
            for j in range(3):
                low = (C * k) // 16 * 16
                high = min((C * k + C + 15) // 16 * 16, WINDOW * C)
                piece = wi[i, j, low:high, :].astype(F32)[C * k - low : C * k - low + C]
                main, tail = parts(piece)
                w4[i, k, 64 * j : 64 * j + 64, :] = main.astype(BF16)
                tails.append(tail)
            tails.append(jnp.zeros((MAIN - 3 * TAIL, HID), F32))
            w4[i, k, 192:256, :] = jnp.concatenate(tails, axis=0).astype(BF16)
            w1[i, k] = w4[i, k].T
        return carry

    lax.fori_loop(0, 3, weights, 0)
    load_wo.wait()
    for i in range(3):
        tails = []
        for j in range(3):
            main, tail = parts(wo[i, j].astype(F32))
            w2[i, 64 * j : 64 * j + 64, :] = main.astype(BF16)
            tails.append(tail)
        tails.append(jnp.zeros((MAIN - 3 * TAIL, HID), F32))
        w2[i, 192:256, :] = jnp.concatenate(tails, axis=0).astype(BF16)
        w2t[i] = w2[i].T

    def stack_chunk(e, g):
        chunk = chunk_of(e, g)
        tails = chunk[64:80, :].astype(F32)
        a, b = ((0, 3), (1, 2))[g]
        stack_into(xs.at[a + 1, e], chunk[0:64, :], tails[0:8], right, left)
        stack_into(xs.at[b + 1, e], chunk[80:144, :], tails[8:16], right, left)

    def stack_halo(e):
        @pl.when(has_up)
        def _():
            lat_copy(0, e, chunk_of(e, 0)).wait_recv()
            stack_into(xs.at[0, e], hb[0, e, 16:80, :], hb[0, e, 0:16, :].astype(F32)[8:16], right, left)

        @pl.when(has_down)
        def _():
            lat_copy(1, e, chunk_of(e, 0)).wait_recv()
            stack_into(xs.at[5, e], hb[1, e, 0:64, :], hb[1, e, 64:80, :].astype(F32)[0:8], right, left)

    for s in range(OWN):
        stack_chunk(OWN + s, 0)
        stack_chunk(OWN + s, 1)
    for s in range(OWN):
        stack_halo(OWN + s)

    def conv_states(t, r, total, picks):
        for e in picks:
            for i in range(3):
                total = total + dot(w1[i, e - t], xs[r + i, e])
        return total

    def phase_own(n, carry):
        t = lax.rem(n, OWN)
        r = n // OWN
        pre[t, r] = conv_states(t, r, bi[...], (2, 3))
        return carry

    lax.fori_loop(0, OWN * ROWS, phase_own, 0)

    tm_copy(0, 1, 0).wait_recv()
    lat_start(1)
    tm_copy(1, 0, 0).wait_recv()
    lat_start(4)
    stack_chunk(1, 0)
    stack_chunk(4, 0)
    tm_copy(0, 0, 0).wait_recv()
    lat_start(0)
    tm_copy(1, 1, 0).wait_recv()
    lat_start(5)
    stack_chunk(0, 0)
    stack_chunk(5, 0)
    tm_copy(0, 1, 1).wait_recv()
    tm_copy(1, 0, 1).wait_recv()
    stack_chunk(1, 1)
    stack_chunk(4, 1)
    stack_halo(1)
    stack_halo(4)

    def phase_near(n, carry):
        t = lax.rem(n, OWN)
        r = n // OWN
        pre[t, r] = conv_states(t, r, pre[t, r], (1, 4))
        return carry

    lax.fori_loop(0, OWN * ROWS, phase_near, 0)
    tm_copy(0, 0, 1).wait_recv()
    tm_copy(1, 1, 1).wait_recv()
    stack_chunk(0, 1)
    stack_chunk(5, 1)
    stack_halo(0)
    stack_halo(5)

    def phase_far(n, carry):
        t = lax.rem(n, OWN)
        r = n // OWN
        v = pre[t, r]
        for i in range(3):
            v = v + dot(w1[i, 4 * t], xs[r + i, 5 * t])
        sig = 0.5 + 0.5 * jnp.tanh(0.5 * v)
        act[r, t] = (v * sig).astype(BF16)
        slope[r, t] = sig * (1.0 + v * (1.0 - sig))
        return carry

    lax.fori_loop(0, OWN * ROWS, phase_far, 0)

    load_ob.wait()

    def score_terms(t, pairs):
        z = None
        for i, r in pairs:
            term = dot(w2[i, 0:ZROWS, :], act[r, t])
            z = term if z is None else z + term
        return combine(z, right, left)

    def pack_score(t, d, kind, main, tail):
        q = 2 * kind + t
        sp[d, 64 * q : 64 * q + 64, :] = main.astype(BF16)
        return tail

    for d, given, kept, r in ((0, ((0, 3),), ((0, 2), (1, 3)), 3), (1, ((2, 0),), ((1, 0), (2, 1)), 0)):
        tails = [None] * 4
        for t in range(OWN):
            main, tail = score_terms(t, given)
            kc[d, t, 0:64, :] = main
            kc[d, t, 64:72, :] = tail
            tails[t] = pack_score(t, d, 0, main, tail)
            main, tail = score_terms(t, kept)
            main = main + bo[0:64, :]
            tail = tail + bo[64:72, :]
            sc[r, t, 0:64, :] = main
            sc[r, t, 64:72, :] = tail
            seen_main, seen_tail = parts(ob[t, :, r, :])
            tails[2 + t] = pack_score(t, d, 1, main - seen_main, tail - seen_tail)
        sp[d, 256:288, :] = jnp.concatenate(tails, axis=0).astype(BF16)

        @pl.when(has_down if d == 0 else has_up)
        def _():
            x2_copy(d).start()

    def finish_row(t, r, main, tail):
        so[t, :, r, :] = jnp.concatenate([main, tail[: C - MAIN]], axis=0)
        seen_main, seen_tail = parts(ob[t, :, r, :])
        stack_into(rs.at[r + 1, t], (main - seen_main).astype(BF16), tail - seen_tail, left, right)

    for t in range(OWN):
        for r in (1, 2):
            main, tail = score_terms(t, tuple((i, r + i - 1) for i in range(3)))
            finish_row(t, r, main + bo[0:64, :], tail + bo[64:72, :])

    for d, r, halo, present in ((0, 0, 0, has_up), (1, 3, 5, has_down)):
        @pl.when(present)
        def _():
            x2_copy(d).wait_recv()
            tails = rp[d, 256:288, :].astype(F32)
            for t in range(OWN):
                sc[r, t, 0:64, :] += rp[d, 64 * t : 64 * t + 64, :].astype(F32)
                sc[r, t, 64:72, :] += tails[8 * t : 8 * t + 8]
                q = 2 + t
                main = kc[1 - d, t, 0:64, :] + rp[d, 64 * q : 64 * q + 64, :].astype(F32)
                tail = kc[1 - d, t, 64:72, :] + tails[8 * q : 8 * q + 8]
                stack_into(rs.at[halo, t], main.astype(BF16), tail, left, right)

    for t in range(OWN):
        for r in (0, 3):
            finish_row(t, r, sc[r, t, 0:64, :], sc[r, t, 64:72, :])

    store_scores = pltpu.make_async_copy(so, scores_out, local.at[4])
    store_scores.start()

    def grad_hidden(t, r):
        total = None
        for i in range(3):
            term = dot(w2t[i], rs[r + 2 - i, t])
            total = term if total is None else total + term
        gp[r + 1, t] = (total * slope[r, t]).astype(BF16)

    def hidden_outer(n, carry):
        grad_hidden(lax.rem(n, OWN), 3 * (n // OWN))
        return carry

    def hidden_inner(n, carry):
        grad_hidden(lax.rem(n, OWN), 1 + n // OWN)
        return carry

    lax.fori_loop(0, 2 * OWN, hidden_outer, 0)

    @pl.when(has_down)
    def _():
        x3_copy(0).start()

    @pl.when(has_up)
    def _():
        x3_copy(1).start()

    lax.fori_loop(0, 2 * OWN, hidden_inner, 0)

    def grad_state(e, r):
        z = None
        for t in range(OWN):
            k = e - t
            if 0 <= k < WINDOW:
                for i in range(3):
                    term = dot(w4[i, k, 0:ZROWS, :], gp[r + 2 - i, t])
                    z = term if z is None else z + term
        return combine(z, left, right)

    def send_row(r):
        for d, e in ((1, 0), (0, 4)):
            main_a, tail_a = grad_state(e, r)
            main_b, tail_b = grad_state(e + 1, r)
            sg[d, r, 0:64, :] = main_a.astype(BF16)
            sg[d, r, 64:80, :] = jnp.concatenate([tail_a, tail_b], axis=0).astype(BF16)
            sg[d, r, 80:144, :] = main_b.astype(BF16)
            g_copy(d, r).start()

    def own_row(r):
        for s in range(OWN):
            main, tail = grad_state(OWN + s, r)
            own[r, s, 0:64, :] = main
            own[r, s, 64:72, :] = tail

    def send_inner(n, carry):
        send_row(1 + n)
        return carry

    def own_inner(n, carry):
        own_row(1 + n)
        return carry

    def send_outer(n, carry):
        send_row(3 * n)
        return carry

    def own_outer(n, carry):
        own_row(3 * n)
        return carry

    lax.fori_loop(0, 2, send_inner, 0)
    lax.fori_loop(0, 2, own_inner, 0)

    @pl.when(has_up)
    def _():
        x3_copy(0).wait_recv()

    @pl.when(has_down)
    def _():
        x3_copy(1).wait_recv()

    lax.fori_loop(0, 2, send_outer, 0)
    lax.fori_loop(0, 2, own_outer, 0)

    for r in (1, 2, 0, 3):
        g_copy(0, r).wait_recv()
        g_copy(1, r).wait_recv()
        tails = rg[0, r, 64:80, :].astype(F32) + rg[1, r, 64:80, :].astype(F32)
        for s in range(OWN):
            low = 80 * s
            main = own[r, s, 0:64, :] + rg[0, r, low : low + 64, :].astype(F32) + rg[1, r, low : low + 64, :].astype(F32)
            tail = own[r, s, 64:72, :] + tails[8 * s : 8 * s + 8]
            go[s, :, r, :] = jnp.concatenate([main, tail[: C - MAIN]], axis=0)
    store_guidance = pltpu.make_async_copy(go, guidance_out, local.at[5])
    store_guidance.start()

    for d in range(2):
        for s in range(OWN):
            for g in range(2):
                tm_copy(d, s, g).wait_send()
        for r in range(ROWS):
            g_copy(d, r).wait_send()

        @pl.when(has_down if d == 0 else has_up)
        def _():
            for e in range(SPAN):
                lat_copy(d, e, chunk_of(e, 0)).wait_send()
            x2_copy(d).wait_send()
            x3_copy(d).wait_send()

    store_scores.wait()
    store_guidance.wait()


def solution(mesh):
    whole = P("tm", None, "lat", None)

    def step(states, observed, conv_in, bias_in, conv_out, bias_out):
        shape = states.shape
        dma = pltpu.SemaphoreType.DMA
        any_space = pl.BlockSpec(memory_space=pl.ANY)
        vmem = pl.BlockSpec(memory_space=pltpu.VMEM)
        return pl.pallas_call(
            kernel,
            out_shape=(jax.ShapeDtypeStruct(shape, F32), jax.ShapeDtypeStruct(shape, F32)),
            in_specs=[any_space, any_space, any_space, vmem, any_space, vmem],
            out_specs=(any_space, any_space),
            scratch_shapes=[
                pltpu.VMEM(shape, F32),
                pltpu.VMEM(shape, F32),
                pltpu.VMEM((3, 3, WINDOW * C, HID), BF16),
                pltpu.VMEM((3, 3, C, HID), BF16),
                pltpu.VMEM((3, WINDOW, 256, HID), BF16),
                pltpu.VMEM((3, WINDOW, HID, 256), BF16),
                pltpu.VMEM((3, 256, HID), BF16),
                pltpu.VMEM((3, HID, 256), BF16),
                pltpu.VMEM((HID, LON), F32),
                pltpu.VMEM((MAIN + TAIL, LON), F32),
                pltpu.VMEM((OWN, 2, CHUNK, LON), BF16),
                pltpu.VMEM((2, OWN, 2, CHUNK, LON), BF16),
                pltpu.VMEM((2, SPAN, EDGE, LON), BF16),
                pltpu.VMEM((ROWS + 2, SPAN, 256, LON), BF16),
                pltpu.VMEM((OWN, ROWS, HID, LON), F32),
                pltpu.VMEM((ROWS, OWN, HID, LON), F32),
                pltpu.VMEM((ROWS, OWN, HID, LON), BF16),
                pltpu.VMEM((2, 4 * (MAIN + TAIL), LON), BF16),
                pltpu.VMEM((2, 4 * (MAIN + TAIL), LON), BF16),
                pltpu.VMEM((2, OWN, MAIN + TAIL, LON), F32),
                pltpu.VMEM((ROWS, OWN, MAIN + TAIL, LON), F32),
                pltpu.VMEM((ROWS + 2, OWN, 256, LON), BF16),
                pltpu.VMEM((ROWS + 2, OWN, HID, LON), BF16),
                pltpu.VMEM((2, ROWS, CHUNK, LON), BF16),
                pltpu.VMEM((2, ROWS, CHUNK, LON), BF16),
                pltpu.VMEM((ROWS, OWN, MAIN + TAIL, LON), F32),
                pltpu.VMEM(shape, F32),
                pltpu.VMEM(shape, F32),
                dma((6,)),
                dma((2, OWN, 2)),
                dma((2, OWN, 2)),
                dma((2, SPAN)),
                dma((2, SPAN)),
                dma((2,)),
                dma((2,)),
                dma((2,)),
                dma((2,)),
                dma((2, ROWS)),
                dma((2, ROWS)),
            ],
            compiler_params=pltpu.CompilerParams(
                collective_id=0, has_side_effects=True, vmem_limit_bytes=60 * 1024 * 1024
            ),
        )(states, observed, jnp.transpose(conv_in, (0, 1, 3, 2)), bias_in, conv_out, bias_out)

    sharded = jax.shard_map(
        step, mesh=mesh, in_specs=(whole, whole, P(), P(), P(), P()), out_specs=(whole, whole), check_vma=False
    )

    def run(*args):
        with jax.sharding.use_abstract_mesh(mesh.abstract_mesh):
            return sharded(*args)

    return run
```

time: 119 us -> 48.1 us (0.40)
  Pallas kernels: 0 us -> 43.3 us
  waiting for transfers between devices: 36.8 us -> 0 us
  matrix products: 31.2 us -> 0 us
  starting transfers between devices: 28.3 us -> 0 us
  local copies, waits for them, and re-layouts: 18.2 us -> 3.92 us
  other arithmetic: 3.02 us -> 0 us
    pallas_call x0 -> x1, Pallas kernels: none -> 43.3 us  [step(): pl.pallas_call(kernel, out_shape=(jax.ShapeDtypeStruct(shape, F32), jax.S...]
    ppermute x12 -> x0, waiting for transfers between devices: 36.8 us -> none  [the longest x5 23.9 us: with_halo(): lax.ppermute(lax.slice_in_dim(block, 0, width, axis=dim), axis, backward)]
    dot_general x36 -> x0, matrix products: 31.2 us -> none  [convolve(): jnp.einsum('oc,tcrw->torw', weights[i, j], band, preferred_element_type=j...]
    ppermute x12 -> x0, starting transfers between devices: 28.3 us -> none  [the longest x5 14.5 us: with_halo(): lax.ppermute(lax.slice_in_dim(block, 0, width, axis=dim), axis, backward)]
    concatenate x1 -> x0, local copies, waits for them, and re-layouts: 6.83 us -> none  [gather_windows(): jnp.concatenate([extended[k:k + count] for k in range(WINDOW)], axis=1)]
    slice x11 -> x0, local copies, waits for them, and re-layouts: 4.55 us -> none  [the longest x6 3.21 us: convolve(): moved = jnp.roll(padded, 1 - j, axis=3)]
    transpose x2 -> x0, local copies, waits for them, and re-layouts: 2.04 us -> none  [flipped(): return jnp.transpose(weights[::-1, ::-1], (0, 1, 3, 2))]
    add x1 -> x0, local copies, waits for them, and re-layouts: 1.82 us -> none  [convolve(): total = term if total is None else total + term]
  transfers between devices with their start and end apart: 12 -> 0, of which waited for: 9 -> 0; matrix products, arithmetic and copies ran while one was open for 5% -> 0% of each run, Pallas kernels for 0% -> 0%
where the time goes in v1:
time: 48.1 us; the launch traced here: 47.9 us
  Pallas kernels  43.3 us (90%)
  local copies, waits for them, and re-layouts  3.92 us (8%)
  between operations  0.64 us (1%)
    pallas_call x1, Pallas kernels, step(): pl.pallas_call(kernel, out_shape=(jax.ShapeDtypeStruct(shape, F32), jax.S...  43.3 us
    unnamed x2, local copies, waits for them, and re-layouts  3.92 us

profile of v1, /device:TPU:97, one launch (start us, length us, event | category | flops | bytes accessed | tf_op | source)
XLA Modules:
  0.0 47.9 jit_solution(41220843846663953)
XLA Ops:
  0.6 43.3 %shard_map.77 = (f32[2,69,4,256]{3,2,1,0:T(4,128)}, f32[2,69,4,256]{3,2,1,0:T(4,128)}) custom-call(f32[2,69,4,256]{3,2,1,0:T(4,128)} %states.1, f32[2,69,4,256]{3,2,1,0:T(4,128)} %observed.1, bf16[3,3,345,256]{3,2,1,0:T(8,128)(2,1)} %bitcast.1, f32[256]{0:T(256)} %bias_in.1, bf16[3,3,69,256]{3,2,1,0:T(8,128)(2,1)} %conv_out.1, f32[69]{0:T(128)} %bias_out.1), custom_call_target="tpu_custom_call" | custom-call | tf_op jit(solution)/shard_map/pallas_call | solution.py:484
  43.9 2.0 %copy.10 = f32[2,69,4,256]{3,2,1,0:T(4,128)} copy(f32[2,69,4,256]{3,2,1,0:T(4,128)} %get-tuple-element.4) | data formatting | bytes 1130496
  45.9 2.0 %copy.11 = f32[2,69,4,256]{3,2,1,0:T(4,128)} copy(f32[2,69,4,256]{3,2,1,0:T(4,128)} %get-tuple-element.5) | data formatting | bytes 1130496

commit v2 on v1

--- a/solution.py
+++ b/solution.py
@@ -32,6 +32,17 @@
     return x[:MAIN], tail
 
 
+def row_of(ref, s, r):
+    return jnp.concatenate([ref[s, pl.ds(ROWS * h + r, C, stride=2 * ROWS), :] for h in range(2)], axis=1)
+
+
+def put_row(ref, s, r, main, tail):
+    for h in range(2):
+        lanes = slice(128 * h, 128 * h + 128)
+        ref[s, pl.ds(ROWS * h + r, MAIN, stride=2 * ROWS), :] = main[:, lanes]
+        ref[s, pl.ds(2 * ROWS * MAIN + ROWS * h + r, C - MAIN, stride=2 * ROWS), :] = tail[: C - MAIN, lanes]
+
+
 def left(x):
     return pltpu.roll(x, LON - 1, axis=1)
 
@@ -55,9 +66,9 @@
 
 
 def kernel(
-    states, observed, conv_in, bias_in, conv_out, bias_out, scores_out, guidance_out,
+    states, observed, conv_in, bias_in, conv_out, bias_out, so, go,
     st, ob, wi, wo, w4, w1, w2, w2t, bi, bo, sbuf, rbuf, hb, xs, pre, slope, act, sp, rp, kc, sc,
-    rs, gp, sg, rg, own, so, go,
+    rs, gp, sg, rg, own,
     local, tm_send, tm_recv, lat_send, lat_recv, x2_send, x2_recv, x3_send, x3_recv, g_send, g_recv,
 ):
     m = lax.axis_index("tm")
@@ -136,8 +147,8 @@
     load_st.wait()
     for g, (a, b) in enumerate(((0, 3), (1, 2))):
         for s in range(OWN):
-            main_a, tail_a = parts(st[s, :, a, :])
-            main_b, tail_b = parts(st[s, :, b, :])
+            main_a, tail_a = parts(row_of(st, s, a))
+            main_b, tail_b = parts(row_of(st, s, b))
             sbuf[s, g, 0:64, :] = main_a.astype(BF16)
             sbuf[s, g, 64:80, :] = jnp.concatenate([tail_a, tail_b], axis=0).astype(BF16)
             sbuf[s, g, 80:144, :] = main_b.astype(BF16)
@@ -249,7 +260,7 @@
         pre[t, r] = conv_states(t, r, bi[...], (2, 3))
         return carry
 
-    lax.fori_loop(0, OWN * ROWS, phase_own, 0)
+    lax.fori_loop(0, OWN * ROWS, phase_own, 0, unroll=True)
 
     tm_copy(0, 1, 0).wait_recv()
     lat_start(1)
@@ -276,7 +287,7 @@
         pre[t, r] = conv_states(t, r, pre[t, r], (1, 4))
         return carry
 
-    lax.fori_loop(0, OWN * ROWS, phase_near, 0)
+    lax.fori_loop(0, OWN * ROWS, phase_near, 0, unroll=True)
     tm_copy(0, 0, 1).wait_recv()
     tm_copy(1, 1, 1).wait_recv()
     stack_chunk(0, 1)
@@ -295,7 +306,7 @@
         slope[r, t] = sig * (1.0 + v * (1.0 - sig))
         return carry
 
-    lax.fori_loop(0, OWN * ROWS, phase_far, 0)
+    lax.fori_loop(0, OWN * ROWS, phase_far, 0, unroll=True)
 
     load_ob.wait()
 
@@ -323,7 +334,7 @@
             tail = tail + bo[64:72, :]
             sc[r, t, 0:64, :] = main
             sc[r, t, 64:72, :] = tail
-            seen_main, seen_tail = parts(ob[t, :, r, :])
+            seen_main, seen_tail = parts(row_of(ob, t, r))
             tails[2 + t] = pack_score(t, d, 1, main - seen_main, tail - seen_tail)
         sp[d, 256:288, :] = jnp.concatenate(tails, axis=0).astype(BF16)
 
@@ -332,14 +343,16 @@
             x2_copy(d).start()
 
     def finish_row(t, r, main, tail):
-        so[t, :, r, :] = jnp.concatenate([main, tail[: C - MAIN]], axis=0)
-        seen_main, seen_tail = parts(ob[t, :, r, :])
+        seen_main, seen_tail = parts(row_of(ob, t, r))
         stack_into(rs.at[r + 1, t], (main - seen_main).astype(BF16), tail - seen_tail, left, right)
 
     for t in range(OWN):
         for r in (1, 2):
             main, tail = score_terms(t, tuple((i, r + i - 1) for i in range(3)))
-            finish_row(t, r, main + bo[0:64, :], tail + bo[64:72, :])
+            main = main + bo[0:64, :]
+            tail = tail + bo[64:72, :]
+            put_row(so, t, r, main, tail)
+            finish_row(t, r, main, tail)
 
     for d, r, halo, present in ((0, 0, 0, has_up), (1, 3, 5, has_down)):
         @pl.when(present)
@@ -358,9 +371,6 @@
         for r in (0, 3):
             finish_row(t, r, sc[r, t, 0:64, :], sc[r, t, 64:72, :])
 
-    store_scores = pltpu.make_async_copy(so, scores_out, local.at[4])
-    store_scores.start()
-
     def grad_hidden(t, r):
         total = None
         for i in range(3):
@@ -376,7 +386,7 @@
         grad_hidden(lax.rem(n, OWN), 1 + n // OWN)
         return carry
 
-    lax.fori_loop(0, 2 * OWN, hidden_outer, 0)
+    lax.fori_loop(0, 2 * OWN, hidden_outer, 0, unroll=True)
 
     @pl.when(has_down)
     def _():
@@ -386,7 +396,11 @@
     def _():
         x3_copy(1).start()
 
-    lax.fori_loop(0, 2 * OWN, hidden_inner, 0)
+    for t in range(OWN):
+        for r in (0, 3):
+            put_row(so, t, r, sc[r, t, 0:64, :], sc[r, t, 64:72, :])
+
+    lax.fori_loop(0, 2 * OWN, hidden_inner, 0, unroll=True)
 
     def grad_state(e, r):
         z = None
@@ -429,8 +443,8 @@
         own_row(3 * n)
         return carry
 
-    lax.fori_loop(0, 2, send_inner, 0)
-    lax.fori_loop(0, 2, own_inner, 0)
+    lax.fori_loop(0, 2, send_inner, 0, unroll=True)
+    lax.fori_loop(0, 2, own_inner, 0, unroll=True)
 
     @pl.when(has_up)
     def _():
@@ -440,8 +454,8 @@
     def _():
         x3_copy(1).wait_recv()
 
-    lax.fori_loop(0, 2, send_outer, 0)
-    lax.fori_loop(0, 2, own_outer, 0)
+    lax.fori_loop(0, 2, send_outer, 0, unroll=True)
+    lax.fori_loop(0, 2, own_outer, 0, unroll=True)
 
     for r in (1, 2, 0, 3):
         g_copy(0, r).wait_recv()
@@ -451,9 +465,7 @@
             low = 80 * s
             main = own[r, s, 0:64, :] + rg[0, r, low : low + 64, :].astype(F32) + rg[1, r, low : low + 64, :].astype(F32)
             tail = own[r, s, 64:72, :] + tails[8 * s : 8 * s + 8]
-            go[s, :, r, :] = jnp.concatenate([main, tail[: C - MAIN]], axis=0)
-    store_guidance = pltpu.make_async_copy(go, guidance_out, local.at[5])
-    store_guidance.start()
+            put_row(go, s, r, main, tail)
 
     for d in range(2):
         for s in range(OWN):
@@ -469,8 +481,16 @@
             x2_copy(d).wait_send()
             x3_copy(d).wait_send()
 
-    store_scores.wait()
-    store_guidance.wait()
+
+def write_out(so, go, scores_out, guidance_out, sems):
+    copies = []
+    for s in range(OWN):
+        copies.append(pltpu.make_async_copy(so.at[s], scores_out.at[s], sems.at[0, s]))
+        copies.append(pltpu.make_async_copy(go.at[s], guidance_out.at[s], sems.at[1, s]))
+    for copy in copies:
+        copy.start()
+    for copy in copies:
+        copy.wait()
 
 
 def solution(mesh):
@@ -479,16 +499,26 @@
     def step(states, observed, conv_in, bias_in, conv_out, bias_out):
         shape = states.shape
         dma = pltpu.SemaphoreType.DMA
-        any_space = pl.BlockSpec(memory_space=pl.ANY)
+        hbm = pl.BlockSpec(memory_space=pltpu.HBM)
         vmem = pl.BlockSpec(memory_space=pltpu.VMEM)
-        return pl.pallas_call(
+        view = (shape[0], shape[1] * shape[2] * 2, 128)
+
+        def seen(x):
+            halves = x.reshape(shape[0], shape[1], shape[2], 2, 128)
+            return jnp.transpose(halves, (0, 1, 3, 2, 4)).reshape(view)
+
+        def unseen(x):
+            halves = x.reshape(shape[0], shape[1], 2, shape[2], 128)
+            return jnp.transpose(halves, (0, 1, 3, 2, 4)).reshape(shape)
+
+        so, go = pl.pallas_call(
             kernel,
-            out_shape=(jax.ShapeDtypeStruct(shape, F32), jax.ShapeDtypeStruct(shape, F32)),
-            in_specs=[any_space, any_space, any_space, vmem, any_space, vmem],
-            out_specs=(any_space, any_space),
+            out_shape=(pltpu.VMEM(view, F32), pltpu.VMEM(view, F32)),
+            in_specs=[hbm, hbm, hbm, vmem, hbm, vmem],
+            out_specs=(vmem, vmem),
             scratch_shapes=[
-                pltpu.VMEM(shape, F32),
-                pltpu.VMEM(shape, F32),
+                pltpu.VMEM(view, F32),
+                pltpu.VMEM(view, F32),
                 pltpu.VMEM((3, 3, WINDOW * C, HID), BF16),
                 pltpu.VMEM((3, 3, C, HID), BF16),
                 pltpu.VMEM((3, WINDOW, 256, HID), BF16),
@@ -513,9 +543,7 @@
                 pltpu.VMEM((2, ROWS, CHUNK, LON), BF16),
                 pltpu.VMEM((2, ROWS, CHUNK, LON), BF16),
                 pltpu.VMEM((ROWS, OWN, MAIN + TAIL, LON), F32),
-                pltpu.VMEM(shape, F32),
-                pltpu.VMEM(shape, F32),
-                dma((6,)),
+                dma((4,)),
                 dma((2, OWN, 2)),
                 dma((2, OWN, 2)),
                 dma((2, SPAN)),
@@ -530,7 +558,17 @@
             compiler_params=pltpu.CompilerParams(
                 collective_id=0, has_side_effects=True, vmem_limit_bytes=60 * 1024 * 1024
             ),
-        )(states, observed, jnp.transpose(conv_in, (0, 1, 3, 2)), bias_in, conv_out, bias_out)
+        )(seen(states), seen(observed), jnp.transpose(conv_in, (0, 1, 3, 2)), bias_in, conv_out, bias_out)
+        so, go = (pltpu.with_memory_space_constraint(x, pltpu.VMEM) for x in (so, go))
+        scores, guidance = pl.pallas_call(
+            write_out,
+            out_shape=(jax.ShapeDtypeStruct(view, F32), jax.ShapeDtypeStruct(view, F32)),
+            in_specs=[vmem, vmem],
+            out_specs=(hbm, hbm),
+            scratch_shapes=[dma((2, OWN))],
+            compiler_params=pltpu.CompilerParams(vmem_limit_bytes=4 * 1024 * 1024),
+        )(so, go)
+        return unseen(scores), unseen(guidance)
 
     sharded = jax.shard_map(
         step, mesh=mesh, in_specs=(whole, whole, P(), P(), P(), P()), out_specs=(whole, whole), check_vma=False

time: 48.1 us -> 40.6 us (0.84)
  local copies, waits for them, and re-layouts: 3.92 us -> 0 us
  Pallas kernels: 43.3 us -> 39.9 us
    unnamed x2 -> x0, local copies, waits for them, and re-layouts: 3.92 us -> none
    pallas_call x1 -> x2, Pallas kernels: 43.3 us -> 39.9 us  [the longest x1 38.8 us: step(): pl.pallas_call(kernel, out_shape=(pltpu.VMEM(view, F32), pltpu.VMEM(view,...]
where the time goes in v2:
time: 40.6 us; the launch traced here: 40.5 us
  Pallas kernels  39.9 us (98%)
  between operations  0.64 us (2%)
    pallas_call x1, Pallas kernels, step(): pl.pallas_call(kernel, out_shape=(pltpu.VMEM(view, F32), pltpu.VMEM(view,...  38.8 us
    pallas_call x1, Pallas kernels, step(): pl.pallas_call(write_out, out_shape=(jax.ShapeDtypeStruct(view, F32), jax...  1.03 us

profile of v2, /device:TPU:97, one launch (start us, length us, event | category | flops | bytes accessed | tf_op | source)
XLA Modules:
  0.0 40.5 jit_solution(4381038792157019426)
XLA Ops:
  0.6 38.8 %shard_map.77 = (f32[2,552,128]{2,1,0:T(8,128)S(1)}, f32[2,552,128]{2,1,0:T(8,128)S(1)}) custom-call(f32[2,552,128]{2,1,0:T(8,128)} %bitcast.22, f32[2,552,128]{2,1,0:T(8,128)} %bitcast.23, bf16[3,3,345,256]{3,2,1,0:T(8,128)(2,1)} %bitcast.21, f32[256]{0:T(256)} %bias_in.1, bf16[3,3,69,256]{3,2,1,0:T(8,128)(2,1)} %conv_out.1, f32[69]{0:T(128)} %bias_out.1), custom_call_target="tpu_custom_call" | custom-call | tf_op jit(solution)/shard_map/pallas_call | solution.py:514
  39.5 1.0 %shard_map.78 = (f32[2,552,128]{2,1,0:T(8,128)}, f32[2,552,128]{2,1,0:T(8,128)}) custom-call(f32[2,552,128]{2,1,0:T(8,128)S(1)} %get-tuple-element.6.so, f32[2,552,128]{2,1,0:T(8,128)S(1)} %get-tuple-element.7.go), custom_call_target="tpu_custom_call" | custom-call | tf_op jit(solution)/shard_map/pallas_call | solution.py:563

commit v3 on v2

--- a/solution.py
+++ b/solution.py
@@ -68,7 +68,7 @@
 def kernel(
     states, observed, conv_in, bias_in, conv_out, bias_out, so, go,
     st, ob, wi, wo, w4, w1, w2, w2t, bi, bo, sbuf, rbuf, hb, xs, pre, slope, act, sp, rp, kc, sc,
-    rs, gp, sg, rg, own,
+    rs, gp, sg, rg, own, near, b1, b2,
     local, tm_send, tm_recv, lat_send, lat_recv, x2_send, x2_recv, x3_send, x3_recv, g_send, g_recv,
 ):
     m = lax.axis_index("tm")
@@ -88,6 +88,10 @@
     load_wi.start()
     load_wo.start()
     load_ob.start()
+    load_b1 = pltpu.make_async_copy(bias_in, b1, local.at[4])
+    load_b2 = pltpu.make_async_copy(bias_out, b2, local.at[5])
+    load_b1.start()
+    load_b2.start()
 
     barrier = pltpu.get_barrier_semaphore()
     pl.semaphore_signal(barrier, inc=1, device_id=(nxt, l), device_id_type=MESH)
@@ -190,8 +194,10 @@
     def _():
         zero_halo(ROWS + 1)
 
-    bi[...] = jnp.broadcast_to(bias_in[...][None, :], (HID, HID)).T
-    row = jnp.concatenate([bias_out[...][None, :], jnp.zeros((1, 128 - C), F32)], axis=1)
+    load_b1.wait()
+    load_b2.wait()
+    bi[...] = jnp.broadcast_to(b1[...][None, :], (HID, HID)).T
+    row = jnp.concatenate([b2[...][None, :], jnp.zeros((1, 128 - C), F32)], axis=1)
     column = jnp.broadcast_to(row, (128, 128)).T
     bo[...] = jnp.concatenate([column[: MAIN + TAIL], column[: MAIN + TAIL]], axis=1)
 
@@ -245,8 +251,6 @@
     for s in range(OWN):
         stack_chunk(OWN + s, 0)
         stack_chunk(OWN + s, 1)
-    for s in range(OWN):
-        stack_halo(OWN + s)
 
     def conv_states(t, r, total, picks):
         for e in picks:
@@ -260,18 +264,20 @@
         pre[t, r] = conv_states(t, r, bi[...], (2, 3))
         return carry
 
-    lax.fori_loop(0, OWN * ROWS, phase_own, 0, unroll=True)
-
+    for s in range(OWN):
+        stack_halo(OWN + s)
     tm_copy(0, 1, 0).wait_recv()
     lat_start(1)
     tm_copy(1, 0, 0).wait_recv()
     lat_start(4)
-    stack_chunk(1, 0)
-    stack_chunk(4, 0)
+    lax.fori_loop(0, OWN * ROWS // 2, phase_own, 0, unroll=True)
     tm_copy(0, 0, 0).wait_recv()
     lat_start(0)
     tm_copy(1, 1, 0).wait_recv()
     lat_start(5)
+    stack_chunk(1, 0)
+    stack_chunk(4, 0)
+    lax.fori_loop(OWN * ROWS // 2, OWN * ROWS, phase_own, 0, unroll=True)
     stack_chunk(0, 0)
     stack_chunk(5, 0)
     tm_copy(0, 1, 1).wait_recv()
@@ -402,60 +408,73 @@
 
     lax.fori_loop(0, 2 * OWN, hidden_inner, 0, unroll=True)
 
-    def grad_state(e, r):
+    def grad_state(e, r, taps=(0, 1, 2)):
         z = None
         for t in range(OWN):
             k = e - t
             if 0 <= k < WINDOW:
-                for i in range(3):
+                for i in taps:
                     term = dot(w4[i, k, 0:ZROWS, :], gp[r + 2 - i, t])
                     z = term if z is None else z + term
         return combine(z, left, right)
 
-    def send_row(r):
-        for d, e in ((1, 0), (0, 4)):
-            main_a, tail_a = grad_state(e, r)
-            main_b, tail_b = grad_state(e + 1, r)
-            sg[d, r, 0:64, :] = main_a.astype(BF16)
-            sg[d, r, 64:80, :] = jnp.concatenate([tail_a, tail_b], axis=0).astype(BF16)
-            sg[d, r, 80:144, :] = main_b.astype(BF16)
+    sides = ((1, 0), (0, 4))
+
+    def pack_row(d, r, pair):
+        (main_a, tail_a), (main_b, tail_b) = pair
+        sg[d, r, 0:64, :] = main_a.astype(BF16)
+        sg[d, r, 64:80, :] = jnp.concatenate([tail_a, tail_b], axis=0).astype(BF16)
+        sg[d, r, 80:144, :] = main_b.astype(BF16)
+
+    def own_rows(rows):
+        for r in rows:
+            for s in range(OWN):
+                main, tail = grad_state(OWN + s, r)
+                own[r, s, 0:64, :] = main
+                own[r, s, 64:72, :] = tail
+
+    for r in (1, 2):
+        for d, e in sides:
+            pack_row(d, r, [grad_state(e + s, r) for s in range(OWN)])
+    for r in (1, 2):
+        for d, e in sides:
             g_copy(d, r).start()
 
-    def own_row(r):
+    for n, (r, taps) in enumerate(((0, (0, 1)), (3, (1, 2)))):
+        for d, e in sides:
+            for s in range(OWN):
+                main, tail = grad_state(e + s, r, taps)
+                near[n, d, s, 0:64, :] = main
+                near[n, d, s, 64:72, :] = tail
+    own_rows((1, 2))
+
+    for n, (r, tap, present) in enumerate(((0, 2, has_up), (3, 0, has_down))):
+        @pl.when(present)
+        def _():
+            x3_copy(n).wait_recv()
+
+        for d, e in sides:
+            pair = []
+            for s in range(OWN):
+                main, tail = grad_state(e + s, r, (tap,))
+                pair.append((main + near[n, d, s, 0:64, :], tail + near[n, d, s, 64:72, :]))
+            pack_row(d, r, pair)
+        for d, e in sides:
+            g_copy(d, r).start()
+
+    own_rows((0, 3))
+
+    for d in range(2):
         for s in range(OWN):
-            main, tail = grad_state(OWN + s, r)
-            own[r, s, 0:64, :] = main
-            own[r, s, 64:72, :] = tail
-
-    def send_inner(n, carry):
-        send_row(1 + n)
-        return carry
-
-    def own_inner(n, carry):
-        own_row(1 + n)
-        return carry
-
-    def send_outer(n, carry):
-        send_row(3 * n)
-        return carry
-
-    def own_outer(n, carry):
-        own_row(3 * n)
-        return carry
-
-    lax.fori_loop(0, 2, send_inner, 0, unroll=True)
-    lax.fori_loop(0, 2, own_inner, 0, unroll=True)
-
-    @pl.when(has_up)
-    def _():
-        x3_copy(0).wait_recv()
-
-    @pl.when(has_down)
-    def _():
-        x3_copy(1).wait_recv()
-
-    lax.fori_loop(0, 2, send_outer, 0, unroll=True)
-    lax.fori_loop(0, 2, own_outer, 0, unroll=True)
+            for g in range(2):
+                tm_copy(d, s, g).wait_send()
+
+        @pl.when(has_down if d == 0 else has_up)
+        def _():
+            for e in range(SPAN):
+                lat_copy(d, e, chunk_of(e, 0)).wait_send()
+            x2_copy(d).wait_send()
+            x3_copy(d).wait_send()
 
     for r in (1, 2, 0, 3):
         g_copy(0, r).wait_recv()
@@ -468,18 +487,8 @@
             put_row(go, s, r, main, tail)
 
     for d in range(2):
-        for s in range(OWN):
-            for g in range(2):
-                tm_copy(d, s, g).wait_send()
         for r in range(ROWS):
             g_copy(d, r).wait_send()
-
-        @pl.when(has_down if d == 0 else has_up)
-        def _():
-            for e in range(SPAN):
-                lat_copy(d, e, chunk_of(e, 0)).wait_send()
-            x2_copy(d).wait_send()
-            x3_copy(d).wait_send()
 
 
 def write_out(so, go, scores_out, guidance_out, sems):
@@ -514,7 +523,7 @@
         so, go = pl.pallas_call(
             kernel,
             out_shape=(pltpu.VMEM(view, F32), pltpu.VMEM(view, F32)),
-            in_specs=[hbm, hbm, hbm, vmem, hbm, vmem],
+            in_specs=[hbm] * 6,
             out_specs=(vmem, vmem),
             scratch_shapes=[
                 pltpu.VMEM(view, F32),
@@ -543,7 +552,10 @@
                 pltpu.VMEM((2, ROWS, CHUNK, LON), BF16),
                 pltpu.VMEM((2, ROWS, CHUNK, LON), BF16),
                 pltpu.VMEM((ROWS, OWN, MAIN + TAIL, LON), F32),
-                dma((4,)),
+                pltpu.VMEM((2, 2, OWN, MAIN + TAIL, LON), F32),
+                pltpu.VMEM((HID,), F32),
+                pltpu.VMEM((C,), F32),
+                dma((6,)),
                 dma((2, OWN, 2)),
                 dma((2, OWN, 2)),
                 dma((2, SPAN)),

time: 40.6 us -> 38.5 us (0.948)
  Pallas kernels: 39.9 us -> 37.7 us
    pallas_call x1, Pallas kernels: 38.8 us -> 36.7 us  [step(): pl.pallas_call(kernel, out_shape=(pltpu.VMEM(view, F32), pltpu.VMEM(view,...]
where the time goes in v3:
time: 38.5 us; the launch traced here: 38.4 us
  Pallas kernels  37.7 us (98%)
  between operations  0.64 us (2%)
    pallas_call x1, Pallas kernels, step(): pl.pallas_call(kernel, out_shape=(pltpu.VMEM(view, F32), pltpu.VMEM(view,...  36.7 us
    pallas_call x1, Pallas kernels, step(): pl.pallas_call(write_out, out_shape=(jax.ShapeDtypeStruct(view, F32), jax...  1.03 us

profile of v3, /device:TPU:97, one launch (start us, length us, event | category | flops | bytes accessed | tf_op | source)
XLA Modules:
  0.0 38.4 jit_solution(15953834620784575211)
XLA Ops:
  0.6 36.7 %shard_map.77 = (f32[2,552,128]{2,1,0:T(8,128)S(1)}, f32[2,552,128]{2,1,0:T(8,128)S(1)}) custom-call(f32[2,552,128]{2,1,0:T(8,128)} %bitcast.22, f32[2,552,128]{2,1,0:T(8,128)} %bitcast.23, bf16[3,3,345,256]{3,2,1,0:T(8,128)(2,1)} %bitcast.21, f32[256]{0:T(256)} %bias_in.1, bf16[3,3,69,256]{3,2,1,0:T(8,128)(2,1)} %conv_out.1, f32[69]{0:T(128)} %bias_out.1), custom_call_target="tpu_custom_call" | custom-call | tf_op jit(solution)/shard_map/pallas_call | solution.py:523
  37.3 1.0 %shard_map.78 = (f32[2,552,128]{2,1,0:T(8,128)}, f32[2,552,128]{2,1,0:T(8,128)}) custom-call(f32[2,552,128]{2,1,0:T(8,128)S(1)} %get-tuple-element.6.so, f32[2,552,128]{2,1,0:T(8,128)S(1)} %get-tuple-element.7.go), custom_call_target="tpu_custom_call" | custom-call | tf_op jit(solution)/shard_map/pallas_call | solution.py:575

commit v4 on v3

--- a/solution.py
+++ b/solution.py
@@ -112,12 +112,12 @@
 
     def tm_copy(d, s, g):
         where = (nxt, l) if d == 0 else (prv, l)
-        return remote(sbuf.at[s, g], rbuf.at[d, s, g], tm_send.at[d, s, g], tm_recv.at[d, s, g], where)
+        return remote(sbuf.at[s, g], rbuf.at[d, s, g], tm_send.at[d], tm_recv.at[d, s, g], where)
 
     def lat_copy(d, e, chunk):
         if d == 0:
-            return remote(chunk.at[pl.ds(MAIN, EDGE)], hb.at[0, e], lat_send.at[0, e], lat_recv.at[0, e], (m, l + 1))
-        return remote(chunk.at[pl.ds(0, EDGE)], hb.at[1, e], lat_send.at[1, e], lat_recv.at[1, e], (m, l - 1))
+            return remote(chunk.at[pl.ds(MAIN, EDGE)], hb.at[0, e], lat_send.at[0], lat_recv.at[0, e], (m, l + 1))
+        return remote(chunk.at[pl.ds(0, EDGE)], hb.at[1, e], lat_send.at[1], lat_recv.at[1, e], (m, l - 1))
 
     def chunk_of(e, g):
         if e < OWN:
@@ -135,9 +135,9 @@
         def _():
             lat_copy(1, e, chunk_of(e, 0)).start()
 
-    def x2_copy(d):
+    def x2_copy(d, t):
         where = (m, l + 1) if d == 0 else (m, l - 1)
-        return remote(sp.at[d], rp.at[d], x2_send.at[d], x2_recv.at[d], where)
+        return remote(sp.at[d, t], rp.at[d, t], x2_send.at[d, t], x2_recv.at[d, t], where)
 
     def x3_copy(d):
         if d == 0:
@@ -146,7 +146,7 @@
 
     def g_copy(d, r):
         where = (nxt, l) if d == 0 else (prv, l)
-        return remote(sg.at[d, r], rg.at[d, r], g_send.at[d, r], g_recv.at[d, r], where)
+        return remote(sg.at[d, r], rg.at[d, r], g_send.at[d], g_recv.at[d, r], where)
 
     load_st.wait()
     for g, (a, b) in enumerate(((0, 3), (1, 2))):
@@ -284,35 +284,37 @@
     tm_copy(1, 0, 1).wait_recv()
     stack_chunk(1, 1)
     stack_chunk(4, 1)
-    stack_halo(1)
-    stack_halo(4)
-
-    def phase_near(n, carry):
-        t = lax.rem(n, OWN)
-        r = n // OWN
+
+    inner = ((0, 1), (1, 1), (0, 2), (1, 2))
+    outer = ((0, 0), (1, 0), (0, 3), (1, 3))
+
+    def phase_near(t, r):
         pre[t, r] = conv_states(t, r, pre[t, r], (1, 4))
-        return carry
-
-    lax.fori_loop(0, OWN * ROWS, phase_near, 0, unroll=True)
-    tm_copy(0, 0, 1).wait_recv()
-    tm_copy(1, 1, 1).wait_recv()
-    stack_chunk(0, 1)
-    stack_chunk(5, 1)
-    stack_halo(0)
-    stack_halo(5)
-
-    def phase_far(n, carry):
-        t = lax.rem(n, OWN)
-        r = n // OWN
+
+    def phase_far(t, r):
         v = pre[t, r]
         for i in range(3):
             v = v + dot(w1[i, 4 * t], xs[r + i, 5 * t])
         sig = 0.5 + 0.5 * jnp.tanh(0.5 * v)
         act[r, t] = (v * sig).astype(BF16)
         slope[r, t] = sig * (1.0 + v * (1.0 - sig))
-        return carry
-
-    lax.fori_loop(0, OWN * ROWS, phase_far, 0, unroll=True)
+
+    for t, r in inner:
+        phase_near(t, r)
+    stack_halo(1)
+    stack_halo(4)
+    for t, r in outer:
+        phase_near(t, r)
+    tm_copy(0, 0, 1).wait_recv()
+    tm_copy(1, 1, 1).wait_recv()
+    stack_chunk(0, 1)
+    stack_chunk(5, 1)
+    for t, r in inner:
+        phase_far(t, r)
+    stack_halo(0)
+    stack_halo(5)
+    for t, r in outer:
+        phase_far(t, r)
 
     load_ob.wait()
 
@@ -323,30 +325,25 @@
             z = term if z is None else z + term
         return combine(z, right, left)
 
-    def pack_score(t, d, kind, main, tail):
-        q = 2 * kind + t
-        sp[d, 64 * q : 64 * q + 64, :] = main.astype(BF16)
-        return tail
-
-    for d, given, kept, r in ((0, ((0, 3),), ((0, 2), (1, 3)), 3), (1, ((2, 0),), ((1, 0), (2, 1)), 0)):
-        tails = [None] * 4
-        for t in range(OWN):
-            main, tail = score_terms(t, given)
+    outer_terms = ((0, ((0, 3),), ((0, 2), (1, 3)), 3), (1, ((2, 0),), ((1, 0), (2, 1)), 0))
+    for t in range(OWN):
+        for d, given, kept, r in outer_terms:
+            main, tail_c = score_terms(t, given)
             kc[d, t, 0:64, :] = main
-            kc[d, t, 64:72, :] = tail
-            tails[t] = pack_score(t, d, 0, main, tail)
+            kc[d, t, 64:72, :] = tail_c
+            sp[d, t, 0:64, :] = main.astype(BF16)
             main, tail = score_terms(t, kept)
             main = main + bo[0:64, :]
             tail = tail + bo[64:72, :]
             sc[r, t, 0:64, :] = main
             sc[r, t, 64:72, :] = tail
             seen_main, seen_tail = parts(row_of(ob, t, r))
-            tails[2 + t] = pack_score(t, d, 1, main - seen_main, tail - seen_tail)
-        sp[d, 256:288, :] = jnp.concatenate(tails, axis=0).astype(BF16)
-
-        @pl.when(has_down if d == 0 else has_up)
-        def _():
-            x2_copy(d).start()
+            sp[d, t, 64:128, :] = (main - seen_main).astype(BF16)
+            sp[d, t, 128:144, :] = jnp.concatenate([tail_c, tail - seen_tail], axis=0).astype(BF16)
+        for d, present in ((0, has_down), (1, has_up)):
+            @pl.when(present)
+            def _():
+                x2_copy(d, t).start()
 
     def finish_row(t, r, main, tail):
         seen_main, seen_tail = parts(row_of(ob, t, r))
@@ -363,14 +360,13 @@
     for d, r, halo, present in ((0, 0, 0, has_up), (1, 3, 5, has_down)):
         @pl.when(present)
         def _():
-            x2_copy(d).wait_recv()
-            tails = rp[d, 256:288, :].astype(F32)
             for t in range(OWN):
-                sc[r, t, 0:64, :] += rp[d, 64 * t : 64 * t + 64, :].astype(F32)
-                sc[r, t, 64:72, :] += tails[8 * t : 8 * t + 8]
-                q = 2 + t
-                main = kc[1 - d, t, 0:64, :] + rp[d, 64 * q : 64 * q + 64, :].astype(F32)
-                tail = kc[1 - d, t, 64:72, :] + tails[8 * q : 8 * q + 8]
+                x2_copy(d, t).wait_recv()
+                tails = rp[d, t, 128:144, :].astype(F32)
+                sc[r, t, 0:64, :] += rp[d, t, 0:64, :].astype(F32)
+                sc[r, t, 64:72, :] += tails[0:8]
+                main = kc[1 - d, t, 0:64, :] + rp[d, t, 64:128, :].astype(F32)
+                tail = kc[1 - d, t, 64:72, :] + tails[8:16]
                 stack_into(rs.at[halo, t], main.astype(BF16), tail, left, right)
 
     for t in range(OWN):
@@ -384,23 +380,17 @@
             total = term if total is None else total + term
         gp[r + 1, t] = (total * slope[r, t]).astype(BF16)
 
-    def hidden_outer(n, carry):
-        grad_hidden(lax.rem(n, OWN), 3 * (n // OWN))
-        return carry
-
     def hidden_inner(n, carry):
         grad_hidden(lax.rem(n, OWN), 1 + n // OWN)
         return carry
 
-    lax.fori_loop(0, 2 * OWN, hidden_outer, 0, unroll=True)
-
-    @pl.when(has_down)
-    def _():
-        x3_copy(0).start()
-
-    @pl.when(has_up)
-    def _():
-        x3_copy(1).start()
+    for d, r, present in ((0, 3, has_down), (1, 0, has_up)):
+        for t in range(OWN):
+            grad_hidden(t, r)
+
+        @pl.when(present)
+        def _():
+            x3_copy(d).start()
 
     for t in range(OWN):
         for r in (0, 3):
@@ -465,15 +455,13 @@
     own_rows((0, 3))
 
     for d in range(2):
-        for s in range(OWN):
-            for g in range(2):
-                tm_copy(d, s, g).wait_send()
+        remote(sbuf, rbuf.at[d], tm_send.at[d], tm_recv.at[d, 0, 0], (nxt, l)).wait_send()
 
         @pl.when(has_down if d == 0 else has_up)
         def _():
-            for e in range(SPAN):
-                lat_copy(d, e, chunk_of(e, 0)).wait_send()
-            x2_copy(d).wait_send()
+            remote(hb.at[d], hb.at[d], lat_send.at[d], lat_recv.at[d, 0], (nxt, l)).wait_send()
+            for t in range(OWN):
+                x2_copy(d, t).wait_send()
             x3_copy(d).wait_send()
 
     for r in (1, 2, 0, 3):
@@ -487,8 +475,7 @@
             put_row(go, s, r, main, tail)
 
     for d in range(2):
-        for r in range(ROWS):
-            g_copy(d, r).wait_send()
+        remote(sg.at[d], rg.at[d], g_send.at[d], g_recv.at[d, 0], (nxt, l)).wait_send()
 
 
 def write_out(so, go, scores_out, guidance_out, sems):
@@ -543,8 +530,8 @@
                 pltpu.VMEM((OWN, ROWS, HID, LON), F32),
                 pltpu.VMEM((ROWS, OWN, HID, LON), F32),
                 pltpu.VMEM((ROWS, OWN, HID, LON), BF16),
-                pltpu.VMEM((2, 4 * (MAIN + TAIL), LON), BF16),
-                pltpu.VMEM((2, 4 * (MAIN + TAIL), LON), BF16),
+                pltpu.VMEM((2, OWN, CHUNK, LON), BF16),
+                pltpu.VMEM((2, OWN, CHUNK, LON), BF16),
                 pltpu.VMEM((2, OWN, MAIN + TAIL, LON), F32),
                 pltpu.VMEM((ROWS, OWN, MAIN + TAIL, LON), F32),
                 pltpu.VMEM((ROWS + 2, OWN, 256, LON), BF16),
@@ -556,15 +543,15 @@
                 pltpu.VMEM((HID,), F32),
                 pltpu.VMEM((C,), F32),
                 dma((6,)),
+                dma((2,)),
                 dma((2, OWN, 2)),
-                dma((2, OWN, 2)),
+                dma((2,)),
                 dma((2, SPAN)),
-                dma((2, SPAN)),
+                dma((2, OWN)),
+                dma((2, OWN)),
                 dma((2,)),
                 dma((2,)),
                 dma((2,)),
-                dma((2,)),
-                dma((2, ROWS)),
                 dma((2, ROWS)),
             ],
             compiler_params=pltpu.CompilerParams(

time: 38.5 us -> 37.8 us (0.982)
  Pallas kernels: 37.7 us -> 37.1 us
    pallas_call x1, Pallas kernels: 36.7 us -> 36 us  [step(): pl.pallas_call(kernel, out_shape=(pltpu.VMEM(view, F32), pltpu.VMEM(view,...]
where the time goes in v4:
time: 37.8 us; the launch traced here: 37.7 us
  Pallas kernels  37.1 us (98%)
  between operations  0.64 us (2%)
    pallas_call x1, Pallas kernels, step(): pl.pallas_call(kernel, out_shape=(pltpu.VMEM(view, F32), pltpu.VMEM(view,...  36 us
    pallas_call x1, Pallas kernels, step(): pl.pallas_call(write_out, out_shape=(jax.ShapeDtypeStruct(view, F32), jax...  1.03 us

profile of v4, /device:TPU:97, one launch (start us, length us, event | category | flops | bytes accessed | tf_op | source)
XLA Modules:
  0.0 37.7 jit_solution(682953627173313677)
XLA Ops:
  0.6 36.0 %shard_map.77 = (f32[2,552,128]{2,1,0:T(8,128)S(1)}, f32[2,552,128]{2,1,0:T(8,128)S(1)}) custom-call(f32[2,552,128]{2,1,0:T(8,128)} %bitcast.22, f32[2,552,128]{2,1,0:T(8,128)} %bitcast.23, bf16[3,3,345,256]{3,2,1,0:T(8,128)(2,1)} %bitcast.21, f32[256]{0:T(256)} %bias_in.1, bf16[3,3,69,256]{3,2,1,0:T(8,128)(2,1)} %conv_out.1, f32[69]{0:T(128)} %bias_out.1), custom_call_target="tpu_custom_call" | custom-call | tf_op jit(solution)/shard_map/pallas_call | solution.py:510
  36.7 1.0 %shard_map.78 = (f32[2,552,128]{2,1,0:T(8,128)}, f32[2,552,128]{2,1,0:T(8,128)}) custom-call(f32[2,552,128]{2,1,0:T(8,128)S(1)} %get-tuple-element.6.so, f32[2,552,128]{2,1,0:T(8,128)S(1)} %get-tuple-element.7.go), custom_call_target="tpu_custom_call" | custom-call | tf_op jit(solution)/shard_map/pallas_call | solution.py:562

commit v5 on v4

--- a/solution.py
+++ b/solution.py
@@ -252,53 +252,54 @@
         stack_chunk(OWN + s, 0)
         stack_chunk(OWN + s, 1)
 
-    def conv_states(t, r, total, picks):
+    inner = ((0, 1), (1, 1), (0, 2), (1, 2))
+    outer = ((0, 0), (1, 0), (0, 3), (1, 3))
+    edge = {0: (1,), 1: (0,), 2: (2,), 3: (1,)}
+    rest = {0: (2, 0), 1: (1, 2), 2: (0, 1), 3: (0, 2)}
+
+    def conv_states(t, r, total, picks, taps=(0, 1, 2)):
         for e in picks:
-            for i in range(3):
+            for i in taps:
                 total = total + dot(w1[i, e - t], xs[r + i, e])
         return total
 
-    def phase_own(n, carry):
-        t = lax.rem(n, OWN)
-        r = n // OWN
+    def phase_own(t, r):
         pre[t, r] = conv_states(t, r, bi[...], (2, 3))
-        return carry
-
+
+    def phase_near(t, r):
+        pre[t, r] = conv_states(t, r, pre[t, r], (1, 4), rest[r])
+
+    def phase_far(t, r):
+        v = conv_states(t, r, pre[t, r], (5 * t,), rest[r])
+        sig = 0.5 + 0.5 * jnp.tanh(0.5 * v)
+        act[r, t] = (v * sig).astype(BF16)
+        slope[r, t] = sig * (1.0 + v * (1.0 - sig))
+
+    for t, r in inner:
+        phase_own(t, r)
     for s in range(OWN):
         stack_halo(OWN + s)
+    for t, r in outer:
+        phase_own(t, r)
+
     tm_copy(0, 1, 0).wait_recv()
     lat_start(1)
     tm_copy(1, 0, 0).wait_recv()
     lat_start(4)
-    lax.fori_loop(0, OWN * ROWS // 2, phase_own, 0, unroll=True)
+    stack_chunk(1, 0)
+    stack_chunk(4, 0)
     tm_copy(0, 0, 0).wait_recv()
     lat_start(0)
     tm_copy(1, 1, 0).wait_recv()
     lat_start(5)
-    stack_chunk(1, 0)
-    stack_chunk(4, 0)
-    lax.fori_loop(OWN * ROWS // 2, OWN * ROWS, phase_own, 0, unroll=True)
     stack_chunk(0, 0)
     stack_chunk(5, 0)
+    for t, r in inner + outer:
+        pre[t, r] = conv_states(t, r, pre[t, r], (1, 4, 5 * t), edge[r])
     tm_copy(0, 1, 1).wait_recv()
     tm_copy(1, 0, 1).wait_recv()
     stack_chunk(1, 1)
     stack_chunk(4, 1)
-
-    inner = ((0, 1), (1, 1), (0, 2), (1, 2))
-    outer = ((0, 0), (1, 0), (0, 3), (1, 3))
-
-    def phase_near(t, r):
-        pre[t, r] = conv_states(t, r, pre[t, r], (1, 4))
-
-    def phase_far(t, r):
-        v = pre[t, r]
-        for i in range(3):
-            v = v + dot(w1[i, 4 * t], xs[r + i, 5 * t])
-        sig = 0.5 + 0.5 * jnp.tanh(0.5 * v)
-        act[r, t] = (v * sig).astype(BF16)
-        slope[r, t] = sig * (1.0 + v * (1.0 - sig))
-
     for t, r in inner:
         phase_near(t, r)
     stack_halo(1)
@@ -426,7 +427,6 @@
     for r in (1, 2):
         for d, e in sides:
             pack_row(d, r, [grad_state(e + s, r) for s in range(OWN)])
-    for r in (1, 2):
         for d, e in sides:
             g_copy(d, r).start()
 

time: 37.8 us -> 37.3 us (0.987)
  Pallas kernels: 37.1 us -> 36.5 us
    pallas_call x1, Pallas kernels: 36 us -> 35.5 us  [step(): pl.pallas_call(kernel, out_shape=(pltpu.VMEM(view, F32), pltpu.VMEM(view,...]
where the time goes in v5:
time: 37.3 us; the launch traced here: 37.2 us
  Pallas kernels  36.5 us (98%)
  between operations  0.64 us (2%)
    pallas_call x1, Pallas kernels, step(): pl.pallas_call(kernel, out_shape=(pltpu.VMEM(view, F32), pltpu.VMEM(view,...  35.5 us
    pallas_call x1, Pallas kernels, step(): pl.pallas_call(write_out, out_shape=(jax.ShapeDtypeStruct(view, F32), jax...  1.03 us

profile of v5, /device:TPU:97, one launch (start us, length us, event | category | flops | bytes accessed | tf_op | source)
XLA Modules:
  0.0 37.2 jit_solution(16459323402885744841)
XLA Ops:
  0.6 35.5 %shard_map.77 = (f32[2,552,128]{2,1,0:T(8,128)S(1)}, f32[2,552,128]{2,1,0:T(8,128)S(1)}) custom-call(f32[2,552,128]{2,1,0:T(8,128)} %bitcast.22, f32[2,552,128]{2,1,0:T(8,128)} %bitcast.23, bf16[3,3,345,256]{3,2,1,0:T(8,128)(2,1)} %bitcast.21, f32[256]{0:T(256)} %bias_in.1, bf16[3,3,69,256]{3,2,1,0:T(8,128)(2,1)} %conv_out.1, f32[69]{0:T(128)} %bias_out.1), custom_call_target="tpu_custom_call" | custom-call | tf_op jit(solution)/shard_map/pallas_call | solution.py:510
  36.1 1.0 %shard_map.78 = (f32[2,552,128]{2,1,0:T(8,128)}, f32[2,552,128]{2,1,0:T(8,128)}) custom-call(f32[2,552,128]{2,1,0:T(8,128)S(1)} %get-tuple-element.6.so, f32[2,552,128]{2,1,0:T(8,128)S(1)} %get-tuple-element.7.go), custom_call_target="tpu_custom_call" | custom-call | tf_op jit(solution)/shard_map/pallas_call | solution.py:562

commit v6 on v5

--- a/solution.py
+++ b/solution.py
@@ -296,28 +296,24 @@
     stack_chunk(5, 0)
     for t, r in inner + outer:
         pre[t, r] = conv_states(t, r, pre[t, r], (1, 4, 5 * t), edge[r])
+    stack_halo(1)
+    stack_halo(4)
     tm_copy(0, 1, 1).wait_recv()
     tm_copy(1, 0, 1).wait_recv()
     stack_chunk(1, 1)
     stack_chunk(4, 1)
-    for t, r in inner:
+    for t, r in inner + outer:
         phase_near(t, r)
-    stack_halo(1)
-    stack_halo(4)
-    for t, r in outer:
-        phase_near(t, r)
+    load_ob.wait()
+    stack_halo(0)
+    stack_halo(5)
     tm_copy(0, 0, 1).wait_recv()
     tm_copy(1, 1, 1).wait_recv()
     stack_chunk(0, 1)
     stack_chunk(5, 1)
-    for t, r in inner:
-        phase_far(t, r)
-    stack_halo(0)
-    stack_halo(5)
-    for t, r in outer:
-        phase_far(t, r)
-
-    load_ob.wait()
+    for t in range(OWN):
+        for r in (0, 1, 3, 2):
+            phase_far(t, r)
 
     def score_terms(t, pairs):
         z = None
@@ -393,10 +389,6 @@
         def _():
             x3_copy(d).start()
 
-    for t in range(OWN):
-        for r in (0, 3):
-            put_row(so, t, r, sc[r, t, 0:64, :], sc[r, t, 64:72, :])
-
     lax.fori_loop(0, 2 * OWN, hidden_inner, 0, unroll=True)
 
     def grad_state(e, r, taps=(0, 1, 2)):
@@ -429,6 +421,10 @@
             pack_row(d, r, [grad_state(e + s, r) for s in range(OWN)])
         for d, e in sides:
             g_copy(d, r).start()
+
+    for t in range(OWN):
+        for r in (0, 3):
+            put_row(so, t, r, sc[r, t, 0:64, :], sc[r, t, 64:72, :])
 
     for n, (r, taps) in enumerate(((0, (0, 1)), (3, (1, 2)))):
         for d, e in sides:

time: 37.3 us -> 37.4 us (level)
  no operation moved by 1% of the time
where the time goes in v6:
time: 37.4 us; the launch traced here: 37.3 us
  Pallas kernels  36.6 us (98%)
  between operations  0.64 us (2%)
    pallas_call x1, Pallas kernels, step(): pl.pallas_call(kernel, out_shape=(pltpu.VMEM(view, F32), pltpu.VMEM(view,...  35.6 us
    pallas_call x1, Pallas kernels, step(): pl.pallas_call(write_out, out_shape=(jax.ShapeDtypeStruct(view, F32), jax...  1.03 us

profile of v6, /device:TPU:97, one launch (start us, length us, event | category | flops | bytes accessed | tf_op | source)
XLA Modules:
  0.0 37.3 jit_solution(15217398437693598962)
XLA Ops:
  0.6 35.6 %shard_map.77 = (f32[2,552,128]{2,1,0:T(8,128)S(1)}, f32[2,552,128]{2,1,0:T(8,128)S(1)}) custom-call(f32[2,552,128]{2,1,0:T(8,128)} %bitcast.22, f32[2,552,128]{2,1,0:T(8,128)} %bitcast.23, bf16[3,3,345,256]{3,2,1,0:T(8,128)(2,1)} %bitcast.21, f32[256]{0:T(256)} %bias_in.1, bf16[3,3,69,256]{3,2,1,0:T(8,128)(2,1)} %conv_out.1, f32[69]{0:T(128)} %bias_out.1), custom_call_target="tpu_custom_call" | custom-call | tf_op jit(solution)/shard_map/pallas_call | solution.py:506
  36.2 1.0 %shard_map.78 = (f32[2,552,128]{2,1,0:T(8,128)}, f32[2,552,128]{2,1,0:T(8,128)}) custom-call(f32[2,552,128]{2,1,0:T(8,128)S(1)} %get-tuple-element.6.so, f32[2,552,128]{2,1,0:T(8,128)S(1)} %get-tuple-element.7.go), custom_call_target="tpu_custom_call" | custom-call | tf_op jit(solution)/shard_map/pallas_call | solution.py:558

commit v7 on v6

--- a/solution.py
+++ b/solution.py
@@ -139,10 +139,10 @@
         where = (m, l + 1) if d == 0 else (m, l - 1)
         return remote(sp.at[d, t], rp.at[d, t], x2_send.at[d, t], x2_recv.at[d, t], where)
 
-    def x3_copy(d):
+    def x3_copy(d, t):
         if d == 0:
-            return remote(gp.at[4], gp.at[0], x3_send.at[0], x3_recv.at[0], (m, l + 1))
-        return remote(gp.at[1], gp.at[5], x3_send.at[1], x3_recv.at[1], (m, l - 1))
+            return remote(gp.at[4, t], gp.at[0, t], x3_send.at[0, t], x3_recv.at[0, t], (m, l + 1))
+        return remote(gp.at[1, t], gp.at[5, t], x3_send.at[1, t], x3_recv.at[1, t], (m, l - 1))
 
     def g_copy(d, r):
         where = (nxt, l) if d == 0 else (prv, l)
@@ -296,13 +296,15 @@
     stack_chunk(5, 0)
     for t, r in inner + outer:
         pre[t, r] = conv_states(t, r, pre[t, r], (1, 4, 5 * t), edge[r])
-    stack_halo(1)
-    stack_halo(4)
     tm_copy(0, 1, 1).wait_recv()
     tm_copy(1, 0, 1).wait_recv()
     stack_chunk(1, 1)
     stack_chunk(4, 1)
-    for t, r in inner + outer:
+    for t, r in inner:
+        phase_near(t, r)
+    stack_halo(1)
+    stack_halo(4)
+    for t, r in outer:
         phase_near(t, r)
     load_ob.wait()
     stack_halo(0)
@@ -381,13 +383,13 @@
         grad_hidden(lax.rem(n, OWN), 1 + n // OWN)
         return carry
 
-    for d, r, present in ((0, 3, has_down), (1, 0, has_up)):
-        for t in range(OWN):
+    for t in range(OWN):
+        for d, r, present in ((0, 3, has_down), (1, 0, has_up)):
             grad_hidden(t, r)
 
-        @pl.when(present)
-        def _():
-            x3_copy(d).start()
+            @pl.when(present)
+            def _():
+                x3_copy(d, t).start()
 
     lax.fori_loop(0, 2 * OWN, hidden_inner, 0, unroll=True)
 
@@ -437,7 +439,8 @@
     for n, (r, tap, present) in enumerate(((0, 2, has_up), (3, 0, has_down))):
         @pl.when(present)
         def _():
-            x3_copy(n).wait_recv()
+            for t in range(OWN):
+                x3_copy(n, t).wait_recv()
 
         for d, e in sides:
             pair = []
@@ -458,7 +461,7 @@
             remote(hb.at[d], hb.at[d], lat_send.at[d], lat_recv.at[d, 0], (nxt, l)).wait_send()
             for t in range(OWN):
                 x2_copy(d, t).wait_send()
-            x3_copy(d).wait_send()
+                x3_copy(d, t).wait_send()
 
     for r in (1, 2, 0, 3):
         g_copy(0, r).wait_recv()
@@ -545,8 +548,8 @@
                 dma((2, SPAN)),
                 dma((2, OWN)),
                 dma((2, OWN)),
-                dma((2,)),
-                dma((2,)),
+                dma((2, OWN)),
+                dma((2, OWN)),
                 dma((2,)),
                 dma((2, ROWS)),
             ],

time: 37.4 us -> 37.3 us (level)
  no operation moved by 1% of the time
where the time goes in v7:
time: 37.3 us; the launch traced here: 37.2 us
  Pallas kernels  36.6 us (98%)
  between operations  0.64 us (2%)
    pallas_call x1, Pallas kernels, step(): pl.pallas_call(kernel, out_shape=(pltpu.VMEM(view, F32), pltpu.VMEM(view,...  35.6 us
    pallas_call x1, Pallas kernels, step(): pl.pallas_call(write_out, out_shape=(jax.ShapeDtypeStruct(view, F32), jax...  1.03 us

profile of v7, /device:TPU:97, one launch (start us, length us, event | category | flops | bytes accessed | tf_op | source)
XLA Modules:
  0.0 37.2 jit_solution(14074553851973302937)
XLA Ops:
  0.6 35.6 %shard_map.77 = (f32[2,552,128]{2,1,0:T(8,128)S(1)}, f32[2,552,128]{2,1,0:T(8,128)S(1)}) custom-call(f32[2,552,128]{2,1,0:T(8,128)} %bitcast.22, f32[2,552,128]{2,1,0:T(8,128)} %bitcast.23, bf16[3,3,345,256]{3,2,1,0:T(8,128)(2,1)} %bitcast.21, f32[256]{0:T(256)} %bias_in.1, bf16[3,3,69,256]{3,2,1,0:T(8,128)(2,1)} %conv_out.1, f32[69]{0:T(128)} %bias_out.1), custom_call_target="tpu_custom_call" | custom-call | tf_op jit(solution)/shard_map/pallas_call | solution.py:509
  36.2 1.0 %shard_map.78 = (f32[2,552,128]{2,1,0:T(8,128)}, f32[2,552,128]{2,1,0:T(8,128)}) custom-call(f32[2,552,128]{2,1,0:T(8,128)S(1)} %get-tuple-element.6.so, f32[2,552,128]{2,1,0:T(8,128)S(1)} %get-tuple-element.7.go), custom_call_target="tpu_custom_call" | custom-call | tf_op jit(solution)/shard_map/pallas_call | solution.py:561

commit v8 on v7

--- a/solution.py
+++ b/solution.py
@@ -384,9 +384,10 @@
         return carry
 
     for t in range(OWN):
-        for d, r, present in ((0, 3, has_down), (1, 0, has_up)):
+        for r in (3, 0):
             grad_hidden(t, r)
-
+    for t in range(OWN):
+        for d, present in ((0, has_down), (1, has_up)):
             @pl.when(present)
             def _():
                 x3_copy(d, t).start()

time: 37.3 us -> 37.2 us (level)
  no operation moved by 1% of the time
where the time goes in v8:
time: 37.2 us; the launch traced here: 37.1 us
  Pallas kernels  36.5 us (98%)
  between operations  0.64 us (2%)
    pallas_call x1, Pallas kernels, step(): pl.pallas_call(kernel, out_shape=(pltpu.VMEM(view, F32), pltpu.VMEM(view,...  35.5 us
    pallas_call x1, Pallas kernels, step(): pl.pallas_call(write_out, out_shape=(jax.ShapeDtypeStruct(view, F32), jax...  1.03 us

profile of v8, /device:TPU:97, one launch (start us, length us, event | category | flops | bytes accessed | tf_op | source)
XLA Modules:
  0.0 37.1 jit_solution(3776067157034407973)
XLA Ops:
  0.6 35.5 %shard_map.77 = (f32[2,552,128]{2,1,0:T(8,128)S(1)}, f32[2,552,128]{2,1,0:T(8,128)S(1)}) custom-call(f32[2,552,128]{2,1,0:T(8,128)} %bitcast.22, f32[2,552,128]{2,1,0:T(8,128)} %bitcast.23, bf16[3,3,345,256]{3,2,1,0:T(8,128)(2,1)} %bitcast.21, f32[256]{0:T(256)} %bias_in.1, bf16[3,3,69,256]{3,2,1,0:T(8,128)(2,1)} %conv_out.1, f32[69]{0:T(128)} %bias_out.1), custom_call_target="tpu_custom_call" | custom-call | tf_op jit(solution)/shard_map/pallas_call | solution.py:510
  36.1 1.0 %shard_map.78 = (f32[2,552,128]{2,1,0:T(8,128)}, f32[2,552,128]{2,1,0:T(8,128)}) custom-call(f32[2,552,128]{2,1,0:T(8,128)S(1)} %get-tuple-element.6.so, f32[2,552,128]{2,1,0:T(8,128)S(1)} %get-tuple-element.7.go), custom_call_target="tpu_custom_call" | custom-call | tf_op jit(solution)/shard_map/pallas_call | solution.py:562
